TPU v7x, 8 devices: a whole 2x2x1 slice. The times are simulated.
8 devices in a mesh: tp: 2 (over z, y), dp: 4 (over x, core).
Axes of the slice: x: 2, y: 2, z: 1, core: 2. Of those that a mesh axis runs over, the one named last changes fastest.
Arguments:
- x_in: bfloat16 [128, 3072], P('dp')
- w_gate: bfloat16 [3072, 8192], P('dp', 'tp')
- w_up: bfloat16 [3072, 8192], P('dp', 'tp')
- w_down: bfloat16 [8192, 3072], P('tp', 'dp')
- dy_in: bfloat16 [128, 3072], P('dp')
Outputs:
- output 1: bfloat16 [128, 3072], P('dp')
- output 2: bfloat16 [128, 3072], P('dp')
- output 3: float32 [3072, 8192], P('dp', 'tp')
- output 4: float32 [3072, 8192], P('dp', 'tp')
- output 5: float32 [8192, 3072], P('tp', 'dp')
All inputs are finite; a program needn't handle non-finite values.
Results may differ from a plain program's by a relative error of at most 0.00101.
Values are sent between devices in bfloat16 or wider.
A program may use at most 1 GiB of HBM per device.

v0:
```python
import jax
import jax.numpy as jnp
from jax import lax
from jax.sharding import PartitionSpec as P


def solution(mesh):
    def device_pass(x_rows, gate_blk, up_blk, down_blk, dy_rows):
        x_cols = lax.all_to_all(x_rows, 'dp', 1, 0, tiled=True)
        gate_part = jnp.dot(x_cols, gate_blk, preferred_element_type=jnp.float32)
        up_part = jnp.dot(x_cols, up_blk, preferred_element_type=jnp.float32)
        gate_pre = lax.psum_scatter(gate_part, 'dp', scatter_dimension=0, tiled=True)
        up_pre = lax.psum_scatter(up_part, 'dp', scatter_dimension=0, tiled=True)
        sig_gate = jax.nn.sigmoid(gate_pre)
        silu_gate = gate_pre * sig_gate
        hidden = (silu_gate * up_pre).astype(jnp.bfloat16)
        hidden_all = lax.all_gather(hidden, 'dp', axis=0, tiled=True)
        out_part = jnp.dot(hidden_all, down_blk, preferred_element_type=jnp.float32)
        y_cols = (x_cols.astype(jnp.float32) + lax.psum(out_part, 'tp')).astype(jnp.bfloat16)
        y_rows = lax.all_to_all(y_cols, 'dp', 0, 1, tiled=True)
        dy_cols = lax.all_to_all(dy_rows, 'dp', 1, 0, tiled=True)
        grad_part = jnp.einsum('td,fd->tf', dy_cols, down_blk, preferred_element_type=jnp.float32)
        grad_h = lax.psum_scatter(grad_part, 'dp', scatter_dimension=0, tiled=True)
        d_gate = (grad_h * up_pre * sig_gate * (1.0 + gate_pre * (1.0 - sig_gate))).astype(jnp.bfloat16)
        d_up = (grad_h * silu_gate).astype(jnp.bfloat16)
        gate_all = lax.all_gather(d_gate, 'dp', axis=0, tiled=True)
        up_all = lax.all_gather(d_up, 'dp', axis=0, tiled=True)
        dx_part = (jnp.einsum('tf,df->td', gate_all, gate_blk, preferred_element_type=jnp.float32)
                   + jnp.einsum('tf,df->td', up_all, up_blk, preferred_element_type=jnp.float32))
        dx_cols = (dy_cols.astype(jnp.float32) + lax.psum(dx_part, 'tp')).astype(jnp.bfloat16)
        dx_rows = lax.all_to_all(dx_cols, 'dp', 0, 1, tiled=True)
        dw_gate = jnp.einsum('td,tf->df', x_cols, gate_all, preferred_element_type=jnp.float32)
        dw_up = jnp.einsum('td,tf->df', x_cols, up_all, preferred_element_type=jnp.float32)
        dw_down = jnp.einsum('tf,td->fd', hidden_all, dy_cols, preferred_element_type=jnp.float32)
        return y_rows, dx_rows, dw_gate, dw_up, dw_down

    row_spec = P('dp', None)
    weight_spec = P('dp', 'tp')
    down_spec = P('tp', 'dp')
    return jax.shard_map(device_pass, mesh=mesh,
                         in_specs=(row_spec, weight_spec, weight_spec, down_spec, row_spec),
                         out_specs=(row_spec, row_spec, weight_spec, weight_spec, down_spec),
                         check_vma=False)
```

profile of v0, /device:TPU:0, one launch (start us, length us, event | category | flops | bytes accessed | tf_op | source)
XLA Modules:
  0.0 243.6 jit_solution(11127828307965340479)
XLA Ops:
  8.2 9.7 %all_to_all.76 = bf16[32,4,768]{2,0,1:T(8,128)(2,1)S(1)} all-to-all(bf16[32,4,768]{2,0,1:T(8,128)(2,1)S(1)} %bitcast.54), channel_id=1, replica_groups=mesh['tp'=2,'dp'=4] {'dp'}, dimensions={1} | all-to-all | bytes 393216 | tf_op jit(solution)/shard_map/all_to_all | solution.py:21
  17.9 6.2 %fusion.4 = f32[128,4096]{1,0:T(8,128)} fusion(bf16[128,768]{1,0:T(8,128)(2,1)S(1)} %bitcast.50, bf16[4096,768]{1,0:T(8,128)(2,1)} %param.8), kind=kOutput, calls=%fused_computation.15 | convolution fusion | flops 805306368 | bytes 8585216 | tf_op jit(solution)/shard_map/td,fd->tf/dot_general | solution.py:22
  24.2 7.7 %all_to_all.77 = bf16[32,4,768]{2,0,1:T(8,128)(2,1)S(1)} all-to-all(bf16[32,4,768]{2,0,1:T(8,128)(2,1)S(1)} %bitcast.55), channel_id=1, replica_groups=mesh['tp'=2,'dp'=4] {'dp'}, dimensions={1} | all-to-all | bytes 393216 | tf_op jit(solution)/shard_map/all_to_all | solution.py:9
  31.9 5.1 %fusion.2 = f32[128,4096]{1,0:T(8,128)} fusion(bf16[128,768]{1,0:T(8,128)(2,1)S(1)} %bitcast.46, bf16[768,4096]{1,0:T(8,128)(2,1)} %param.7), kind=kOutput, calls=%fused_computation.13 | convolution fusion | flops 805306368 | bytes 8585216 | tf_op jit(solution)/shard_map/dot_general | solution.py:11
  37.1 5.1 %fusion.1 = f32[128,4096]{1,0:T(8,128)} fusion(bf16[128,768]{1,0:T(8,128)(2,1)S(1)} %bitcast.47, bf16[768,4096]{1,0:T(8,128)(2,1)} %param.6), kind=kOutput, calls=%fused_computation.12 | convolution fusion | flops 805306368 | bytes 8585216 | tf_op jit(solution)/shard_map/dot_general | solution.py:10
  42.2 7.6 %reduce-scatter.8.cloned.1.call-done = f32[32,4096]{1,0:T(8,128)} async-done(((f32[128,4096]{1,0:T(8,128)}), f32[32,4096]{1,0:T(8,128)}) %reduce-scatter.8.cloned.1.call-update) | async-done | bytes 524304 | tf_op jit(solution)/shard_map/reduce_scatter | solution.py:23
  49.9 28.6 %reduce-scatter.6.cloned.1.call-done = f32[32,4096]{1,0:T(8,128)} async-done(((f32[128,4096]{1,0:T(8,128)}), f32[32,4096]{1,0:T(8,128)}) %reduce-scatter.6.cloned.1.call-update) | async-done | bytes 524304 | tf_op jit(solution)/shard_map/reduce_scatter | solution.py:13
  78.5 28.6 %reduce-scatter.4.cloned.1.call-done = f32[32,4096]{1,0:T(8,128)} async-done(((f32[128,4096]{1,0:T(8,128)}), f32[32,4096]{1,0:T(8,128)}) %reduce-scatter.4.cloned.1.call-update) | async-done | bytes 524304 | tf_op jit(solution)/shard_map/reduce_scatter | solution.py:12
  107.1 2.5 %multiply_convert_fusion = (bf16[32,4096]{1,0:T(8,128)(2,1)}, bf16[32,4096]{1,0:T(8,128)(2,1)}, bf16[32,4096]{1,0:T(8,128)(2,1)}) fusion(f32[32,4096]{1,0:T(8,128)} %reduce-scatter.8.cloned.1.call-done, f32[32,4096]{1,0:T(8,128)} %reduce-scatter.4.cloned.1.call-done, f32[32,4096]{1,0:T(8,128)} %reduce-scatter.6.cloned.1.call-done), kind=kLoop, calls=%fused_computation.3 | loop fusion | flops 1966080 | bytes 2359296 | tf_op jit(solution)/shard_map/convert_element_type | solution.py:25
  110.8 12.7 %all-gather.4.cloned.1.call-done = bf16[128,4096]{1,0:T(8,128)(2,1)} async-done(((bf16[32,4096]{1,0:T(8,128)(2,1)}), bf16[128,4096]{1,0:T(8,128)(2,1)}) %all-gather.4.cloned.1.call-update) | async-done | bytes 1048592 | tf_op jit(solution)/shard_map/all_gather | solution.py:17
  123.5 4.9 %fusion.3 = f32[128,768]{1,0:T(8,128)} fusion(bf16[128,4096]{1,0:T(8,128)(2,1)} %all-gather.4.cloned.1.call-done, bf16[4096,768]{1,0:T(8,128)(2,1)} %param.8), kind=kOutput, calls=%fused_computation.14 | convolution fusion | flops 805306368 | bytes 7733248 | tf_op jit(solution)/shard_map/dot_general | solution.py:18
  128.4 10.9 %all-gather.6.cloned.1.call-done = bf16[128,4096]{1,0:T(8,128)(2,1)} async-done(((bf16[32,4096]{1,0:T(8,128)(2,1)}), bf16[128,4096]{1,0:T(8,128)(2,1)}) %all-gather.6.cloned.1.call-update) | async-done | bytes 1048592 | tf_op jit(solution)/shard_map/all_gather | solution.py:26
  139.2 5.3 %fusion.5 = f32[128,768]{1,0:T(8,128)S(1)} fusion(bf16[128,4096]{1,0:T(8,128)(2,1)} %all-gather.6.cloned.1.call-done, bf16[768,4096]{1,0:T(8,128)(2,1)} %param.6), kind=kOutput, calls=%fused_computation.16 | convolution fusion | flops 805306368 | bytes 7733248 | tf_op jit(solution)/shard_map/tf,df->td/dot_general | solution.py:28
  144.6 10.4 %all-gather.8.cloned.1.call-done = bf16[128,4096]{1,0:T(8,128)(2,1)} async-done(((bf16[32,4096]{1,0:T(8,128)(2,1)}), bf16[128,4096]{1,0:T(8,128)(2,1)}) %all-gather.8.cloned.1.call-update) | async-done | bytes 1048592 | tf_op jit(solution)/shard_map/all_gather | solution.py:27
  154.9 6.2 %convolution_add_fusion = f32[128,768]{1,0:T(8,128)} fusion(f32[128,768]{1,0:T(8,128)S(1)} %fusion.5, bf16[128,4096]{1,0:T(8,128)(2,1)} %all-gather.8.cloned.1.call-done, bf16[768,4096]{1,0:T(8,128)(2,1)} %param.7), kind=kOutput, calls=%fused_computation.2 | convolution fusion | flops 805404672 | bytes 8126464 | tf_op jit(solution)/shard_map/tf,df->td/dot_general | solution.py:29
  161.1 6.6 %convolution_bitcast_fusion = f32[768,4096]{0,1:T(8,128)} fusion(bf16[128,4096]{1,0:T(8,128)(2,1)S(1)} %copy-done.2, bf16[128,768]{1,0:T(8,128)(2,1)S(1)} %bitcast.48), kind=kOutput, calls=%fused_computation | convolution fusion | flops 805306368 | bytes 13828096 | tf_op jit(solution)/shard_map/td,tf->df/dot_general | solution.py:33
  167.7 6.4 %convolution_bitcast_fusion.1 = f32[768,4096]{0,1:T(8,128)} fusion(bf16[128,4096]{1,0:T(8,128)(2,1)S(1)} %copy-done.1, bf16[128,768]{1,0:T(8,128)(2,1)S(1)} %bitcast.49), kind=kOutput, calls=%fused_computation.1 | convolution fusion | flops 805306368 | bytes 13828096 | tf_op jit(solution)/shard_map/td,tf->df/dot_general | solution.py:32
  174.1 15.7 %all-reduce.3.cloned.1.call-done = (f32[128,768]{1,0:T(8,128)}, f32[128,768]{1,0:T(8,128)}) async-done(((f32[128,768]{1,0:T(8,128)}, f32[128,768]{1,0:T(8,128)}), (f32[128,768]{1,0:T(8,128)}, f32[128,768]{1,0:T(8,128)})) %all-reduce.3.cloned.1.call-update) | async-done | bytes 786448 | tf_op jit(solution)/shard_map/psum | solution.py:19
  191.5 3.5 %all-to-all-start.1 = ((bf16[4,32,768]{2,1,0:T(8,128)(2,1)}), bf16[4,32,768]{2,1,0:T(8,128)(2,1)S(1)}, u32[]{:S(2)}, u32[]{:S(2)}) async-start(bf16[4,32,768]{2,1,0:T(8,128)(2,1)} %bitcast.3), calls=%async_computation.3 | async-start | bytes 393216 | tf_op jit(solution)/shard_map/all_to_all | solution.py:20
  196.8 3.3 %all-to-all-done.1 = bf16[4,32,768]{2,1,0:T(8,128)(2,1)S(1)} async-done(((bf16[4,32,768]{2,1,0:T(8,128)(2,1)}), bf16[4,32,768]{2,1,0:T(8,128)(2,1)S(1)}, u32[]{:S(2)}, u32[]{:S(2)}) %all-to-all-start.1) | async-done | bytes 196640 | tf_op jit(solution)/shard_map/all_to_all | solution.py:20
  200.1 3.4 %all-to-all-start.3 = ((bf16[4,32,768]{2,1,0:T(8,128)(2,1)}), bf16[4,32,768]{2,1,0:T(8,128)(2,1)S(1)}, u32[]{:S(2)}, u32[]{:S(2)}) async-start(bf16[4,32,768]{2,1,0:T(8,128)(2,1)} %bitcast.8), calls=%async_computation.6 | async-start | bytes 393216 | tf_op jit(solution)/shard_map/all_to_all | solution.py:31
  203.5 6.6 %fusion.6 = f32[4096,768]{1,0:T(8,128)} fusion(bf16[128,4096]{1,0:T(8,128)(2,1)S(1)} %copy-done, bf16[128,768]{1,0:T(8,128)(2,1)S(1)} %bitcast.51), kind=kOutput, calls=%fused_computation.17 | convolution fusion | flops 805306368 | bytes 13828096 | tf_op jit(solution)/shard_map/tf,td->fd/dot_general | solution.py:34
  210.1 12.6 %copy.15 = f32[768,4096]{1,0:T(8,128)} copy(f32[768,4096]{0,1:T(8,128)} %convolution_bitcast_fusion) | data formatting | bytes 25165824
  222.7 12.6 %copy.14 = f32[768,4096]{1,0:T(8,128)} copy(f32[768,4096]{0,1:T(8,128)} %convolution_bitcast_fusion.1) | data formatting | bytes 25165824
  (29 shorter events, 7.2 us)
Async XLA Ops:
  7.2 17.0 %copy-start.3 = (bf16[32,3072]{1,0:T(8,128)(2,1)S(1)}, bf16[32,3072]{1,0:T(8,128)(2,1)}, u32[]{:S(2)}) copy-start(bf16[32,3072]{1,0:T(8,128)(2,1)} %param.5) | copy-start | bytes 589828
  7.2 42.7 %reduce-scatter.8.cloned.1.call-start = ((), (), s32[]{:S(2)}) async-start(), calls=%async_computation.10 | async-start | bytes 2621440 | tf_op jit(solution)/shard_map/reduce_scatter | solution.py:23
  24.1 54.4 %reduce-scatter.6.cloned.1.call-start = ((), (), s32[]{:S(2)}) async-start(), calls=%async_computation.8 | async-start | bytes 2621440 | tf_op jit(solution)/shard_map/reduce_scatter | solution.py:13
  37.0 70.1 %reduce-scatter.4.cloned.1.call-start = ((), (), s32[]{:S(2)}) async-start(), calls=%async_computation.7 | async-start | bytes 2621440 | tf_op jit(solution)/shard_map/reduce_scatter | solution.py:12
  42.2 81.3 %all-gather.4.cloned.1.call-start = ((), (), s32[]{:S(2)}) async-start(), calls=%async_computation.9 | async-start | bytes 1310720 | tf_op jit(solution)/shard_map/all_gather | solution.py:17
  109.6 29.6 %all-gather.6.cloned.1.call-start = ((), (), s32[]{:S(2)}) async-start(), calls=%async_computation.11 | async-start | bytes 1310720 | tf_op jit(solution)/shard_map/all_gather | solution.py:26
  110.2 44.7 %all-gather.8.cloned.1.call-start = ((), (), s32[]{:S(2)}) async-start(), calls=%async_computation.12 | async-start | bytes 1310720 | tf_op jit(solution)/shard_map/all_gather | solution.py:27
  110.8 79.0 %all-reduce.3.cloned.1.call-start = ((), (), s32[]{:S(2)}) async-start(), calls=%async_computation.13 | async-start | bytes 1572864 | tf_op jit(solution)/shard_map/psum | solution.py:19
  154.9 6.2 %copy-start.2 = (bf16[128,4096]{1,0:T(8,128)(2,1)S(1)}, bf16[128,4096]{1,0:T(8,128)(2,1)}, u32[]{:S(2)}) copy-start(bf16[128,4096]{1,0:T(8,128)(2,1)} %all-gather.8.cloned.1.call-done) | copy-start | bytes 3145732
  161.1 6.6 %copy-start.1 = (bf16[128,4096]{1,0:T(8,128)(2,1)S(1)}, bf16[128,4096]{1,0:T(8,128)(2,1)}, u32[]{:S(2)}) copy-start(bf16[128,4096]{1,0:T(8,128)(2,1)} %all-gather.6.cloned.1.call-done) | copy-start | bytes 3145732
  167.7 35.8 %copy-start = (bf16[128,4096]{1,0:T(8,128)(2,1)S(1)}, bf16[128,4096]{1,0:T(8,128)(2,1)}, u32[]{:S(2)}) copy-start(bf16[128,4096]{1,0:T(8,128)(2,1)} %all-gather.4.cloned.1.call-done) | copy-start | bytes 3145732
  191.5 8.6 %all-to-all-start.1 = ((bf16[4,32,768]{2,1,0:T(8,128)(2,1)}), bf16[4,32,768]{2,1,0:T(8,128)(2,1)S(1)}, u32[]{:S(2)}, u32[]{:S(2)}) async-start(bf16[4,32,768]{2,1,0:T(8,128)(2,1)} %bitcast.3), calls=%async_computation.3 | async-start | bytes 393216 | tf_op jit(solution)/shard_map/all_to_all | solution.py:20
  200.1 35.9 %all-to-all-start.3 = ((bf16[4,32,768]{2,1,0:T(8,128)(2,1)}), bf16[4,32,768]{2,1,0:T(8,128)(2,1)S(1)}, u32[]{:S(2)}, u32[]{:S(2)}) async-start(bf16[4,32,768]{2,1,0:T(8,128)(2,1)} %bitcast.8), calls=%async_computation.6 | async-start | bytes 393216 | tf_op jit(solution)/shard_map/all_to_all | solution.py:31
Sparse Core Ops, SparseCore 0:
  24.3 25.5 reduce-scatter.7
  52.9 25.5 reduce-scatter.5
  81.6 25.5 reduce-scatter.3
  109.7 13.7 all-gather.3
  125.4 13.7 all-gather.5
  141.2 13.7 all-gather.7
  161.2 28.5 all-reduce.2
where the time goes:
time: 244 us
  waiting for transfers between devices  119 us (49%)
  matrix products  52.3 us (21%)
  local copies, waits for them, and re-layouts  27.6 us (11%)
  blocking collectives  17.4 us (7%)
  between operations  14.2 us (6%)
  starting transfers between devices  7.19 us (3%)
  other arithmetic  5.88 us (2%)
    reduce_scatter x1, waiting for transfers between devices, device_pass(): lax.psum_scatter(gate_part, 'dp', scatter_dimension=0, tiled=True)  28.6 us
    reduce_scatter x1, waiting for transfers between devices, device_pass(): up_pre = lax.psum_scatter(up_part, 'dp', scatter_dimension=0, tiled=True)  28.6 us
    unnamed x10, local copies, waits for them, and re-layouts  25.2 us
    psum x1, waiting for transfers between devices, device_pass(): lax.psum(out_part, 'tp')  15.7 us
    all_gather x1, waiting for transfers between devices, device_pass(): hidden_all = lax.all_gather(hidden, 'dp', axis=0, tiled=True)  12.7 us
    all_gather x1, waiting for transfers between devices, device_pass(): gate_all = lax.all_gather(d_gate, 'dp', axis=0, tiled=True)  10.9 us
    all_gather x1, waiting for transfers between devices, device_pass(): up_all = lax.all_gather(d_up, 'dp', axis=0, tiled=True)  10.4 us
    all_to_all x1, blocking collectives, device_pass(): dy_cols = lax.all_to_all(dy_rows, 'dp', 1, 0, tiled=True)  9.71 us
  transfers between devices with their start and end apart: 9, of which 8 were waited for; matrix products, arithmetic and copies ran while one was open for 28% of the time, Pallas kernels for 0%

commit v1 on v0

v1 whole, which is shorter than its diff:
```python
import functools

import jax
import jax.numpy as jnp
from jax import lax
from jax.experimental import pallas as pl
from jax.experimental.pallas import tpu as pltpu
from jax.sharding import PartitionSpec as P

MESH = pl.DeviceIdType.MESH
F32 = jnp.float32
BF16 = jnp.bfloat16
CHUNK = 512
SHARDS = 4
OWN, FAR, SIB, DIAG = 0, 1, 2, 3


def _dot(lhs, rhs, lhs_dim, rhs_dim):
    return lax.dot_general(lhs, rhs, (((lhs_dim,), (rhs_dim,)), ((), ())), preferred_element_type=F32)


def exchange_kernel(chunks, x_hbm, gate_hbm, up_hbm, down_hbm, dy_hbm,
                    xc_out, dyc_out, hid_out, grad_out, y_out, dx_out,
                    x_own, dy_own, xc, dyc, gate, up, down,
                    ab_keep, ab_give, ab_got, g_keep, g_give, g_got,
                    ab_send, ab_recv, g_send, g_recv, hid, grad,
                    y_acc, dx_acc, y_peer, dx_peer, y_sum, dx_sum, y_stage, dx_stage,
                    in_sem, w_sem, tok_ss, tok_rs, core_ss, core_rs, link_ss, link_rs,
                    hid_ss, hid_rs, grad_ss, grad_rs, tp_ss, tp_rs, row_ss, row_rs, out_sem):
    tp = lax.axis_index('tp')
    dp = lax.axis_index('dp')
    sib = dp + 1 - 2 * lax.rem(dp, 2)
    far = lax.rem(dp + 2, SHARDS)
    diag = lax.rem(sib + 2, SHARDS)
    peers = {FAR: far, SIB: sib, DIAG: diag}
    width = xc.shape[-1]

    def remote(src, dst, ss, rs, **device):
        return pltpu.make_async_remote_copy(src_ref=src, dst_ref=dst, send_sem=ss, recv_sem=rs,
                                            device_id=device, device_id_type=MESH)

    def cols(i):
        return pl.ds(pl.multiple_of(i * width, width), width)

    def span(c):
        return pl.ds(pl.multiple_of(c * CHUNK, CHUNK), CHUNK)

    def load_gate(c):
        return pltpu.make_async_copy(gate_hbm.at[:, span(c)], gate.at[c], w_sem.at[0, c])

    def load_up(c):
        return pltpu.make_async_copy(up_hbm.at[:, span(c)], up.at[c], w_sem.at[1, c])

    def load_down(c):
        return pltpu.make_async_copy(down_hbm.at[span(c)], down.at[c], w_sem.at[2, c])

    tokens = ((x_hbm, x_own, xc, 0), (dy_hbm, dy_own, dyc, 1))
    stage_in = [pltpu.make_async_copy(h, v, in_sem.at[i]) for h, v, _, i in tokens]
    keep_in = [pltpu.make_async_copy(h.at[:, :, cols(dp)], s.at[OWN], in_sem.at[2 + i]) for h, _, s, i in tokens]
    for copy in stage_in + keep_in:
        copy.start()
    for c in range(chunks):
        load_gate(c).start()
        load_up(c).start()
    for c in range(chunks):
        load_down(c).start()

    barrier = pltpu.get_barrier_semaphore()
    for p in (FAR, SIB, DIAG):
        pl.semaphore_signal(barrier, inc=1, device_id={'dp': peers[p]}, device_id_type=MESH)
        pl.semaphore_signal(barrier, inc=1, device_id={'dp': peers[p], 'tp': 1 - tp}, device_id_type=MESH)
    pl.semaphore_signal(barrier, inc=1, device_id={'tp': 1 - tp}, device_id_type=MESH)
    pl.semaphore_wait(barrier, 2 * SHARDS - 1)

    token_copies = []
    for _, own, slots, i in tokens:
        stage_in[i].wait()
        for p in (FAR, DIAG, SIB):
            copy = remote(own.at[:, :, cols(peers[p])], slots.at[p], tok_ss.at[i, p], tok_rs.at[i, p], dp=peers[p])
            copy.start()
            token_copies.append(copy)
        token_copies.append(None)

    def core_ab(c):
        return remote(ab_give.at[c], ab_got.at[c], core_ss.at[0, c], core_rs.at[0, c], dp=sib)

    def core_g(c):
        return remote(g_give.at[c], g_got.at[c], core_ss.at[1, c], core_rs.at[1, c], dp=sib)

    def link_ab(c):
        return remote(ab_send.at[c], ab_recv.at[c], link_ss.at[0, c], link_rs.at[0, c], dp=far)

    def link_g(c):
        return remote(g_send.at[c], g_recv.at[c], link_ss.at[1, c], link_rs.at[1, c], dp=far)

    rows = 2 * x_own.shape[1]
    all_rows = SHARDS * rows

    def put(part, keep, give, index):
        part = part.reshape(SHARDS, rows, CHUNK)
        keep[index] = part[:2]
        give[index] = part[2:]

    def send_ab(c):
        core_ab(c).wait_recv()
        ab_send[c] = ab_keep[c, :, 1] + ab_got[c, :, 1]
        link_ab(c).start()

    def send_g(c):
        core_g(c).wait_recv()
        g_send[c] = g_keep[c, 1] + g_got[c, 1]
        link_g(c).start()

    keep_in[0].wait()
    for copy in token_copies[:3]:
        copy.wait_recv()

    def part_ab(c, carry):
        tok = xc[...].reshape(all_rows, width)
        load_gate(c).wait()
        put(_dot(tok, gate[c], 1, 0), ab_keep, ab_give, (c, 0))
        load_up(c).wait()
        put(_dot(tok, up[c], 1, 0), ab_keep, ab_give, (c, 1))
        core_ab(c).start()

        @pl.when(c > 0)
        def _():
            send_ab(c - 1)
        return carry

    lax.fori_loop(0, chunks, part_ab, 0)
    send_ab(chunks - 1)

    keep_in[1].wait()
    for copy in token_copies[4:7]:
        copy.wait_recv()

    def part_g(c, carry):
        tok = dyc[...].reshape(all_rows, width)
        load_down(c).wait()
        put(_dot(tok, down[c], 1, 1), g_keep, g_give, (c,))
        core_g(c).start()

        @pl.when(c > 0)
        def _():
            send_g(c - 1)
        return carry

    lax.fori_loop(0, chunks, part_g, 0)
    send_g(chunks - 1)

    keep_out = [pltpu.make_async_copy(xc, xc_out, out_sem.at[0]), pltpu.make_async_copy(dyc, dyc_out, out_sem.at[1])]
    for copy in keep_out:
        copy.start()

    def hid_far(c):
        return remote(hid.at[c, OWN], hid.at[c, FAR], hid_ss.at[0, c], hid_rs.at[0, c], dp=far)

    def hid_sib(c):
        return remote(hid.at[c, OWN], hid.at[c, SIB], hid_ss.at[1, c], hid_rs.at[1, c], dp=sib)

    def hid_fwd(c):
        return remote(hid.at[c, FAR], hid.at[c, DIAG], hid_ss.at[2, c], hid_rs.at[2, c], dp=sib)

    def grad_far(c):
        return remote(grad.at[c, OWN], grad.at[c, FAR], grad_ss.at[0, c], grad_rs.at[0, c], dp=far)

    def grad_sib(c):
        return remote(grad.at[c, OWN], grad.at[c, SIB], grad_ss.at[1, c], grad_rs.at[1, c], dp=sib)

    def grad_fwd(c):
        return remote(grad.at[c, FAR], grad.at[c, DIAG], grad_ss.at[2, c], grad_rs.at[2, c], dp=sib)

    def hid_save(c):
        return pltpu.make_async_copy(hid.at[c], hid_out.at[c], out_sem.at[2 + c])

    def grad_save(c):
        return pltpu.make_async_copy(grad.at[c], grad_out.at[c], out_sem.at[2 + chunks + c])

    def form_hidden(c, carry):
        link_ab(c).wait_recv()
        total = ab_keep[c, :, 0] + ab_got[c, :, 0] + ab_recv[c]
        ab_keep[c, :, 0] = total
        a, b = total[0], total[1]
        hid[c, OWN] = (a * jax.nn.sigmoid(a) * b).astype(BF16)
        hid_far(c).start()
        hid_sib(c).start()
        return carry

    lax.fori_loop(0, chunks, form_hidden, 0)

    def form_grads(c, carry):
        link_g(c).wait_recv()
        g = g_keep[c, 0] + g_got[c, 0] + g_recv[c]
        a, b = ab_keep[c, 0, 0], ab_keep[c, 1, 0]
        s = jax.nn.sigmoid(a)
        grad[c, OWN, 0] = (g * b * s * (1.0 + a * (1.0 - s))).astype(BF16)
        grad[c, OWN, 1] = (g * (a * s)).astype(BF16)
        grad_far(c).start()
        grad_sib(c).start()
        return carry

    lax.fori_loop(0, chunks, form_grads, 0)

    y_acc[...] = jnp.zeros_like(y_acc)
    dx_acc[...] = jnp.zeros_like(dx_acc)

    def use_hidden(c):
        hid_sib(c).wait_recv()
        hid_fwd(c).wait_recv()
        hid_save(c).start()
        y_acc[...] += _dot(hid[c].reshape(all_rows, CHUNK), down[c], 1, 0).reshape(y_acc.shape)

    def take_hidden(c, carry):
        hid_far(c).wait_recv()
        hid_fwd(c).start()

        @pl.when(c > 0)
        def _():
            use_hidden(c - 1)
        return carry

    lax.fori_loop(0, chunks, take_hidden, 0)
    use_hidden(chunks - 1)

    def tp_copy(acc, peer, i):
        return remote(acc.at[:, 1 - tp], peer, tp_ss.at[i], tp_rs.at[i], tp=1 - tp)

    def row_copies(total, stage, i):
        out = []
        for p in (FAR, DIAG, SIB):
            out.append(remote(total.at[p], stage.at[p, 0], row_ss.at[i, p, 0], row_rs.at[i, p, 0], dp=peers[p]))
            out.append(remote(total.at[p], stage.at[p, 1], row_ss.at[i, p, 1], row_rs.at[i, p, 1],
                              dp=peers[p], tp=1 - tp))
        out.append(remote(total.at[OWN], stage.at[OWN, 1], row_ss.at[i, OWN, 1], row_rs.at[i, OWN, 1], tp=1 - tp))
        return out

    def finish(tok, acc, peer, total, stage, i):
        tp_copy(acc, peer, i).wait()
        rows_out = (tok[:, tp].astype(F32) + (acc[:, tp] + peer[...])).astype(BF16)
        total[...] = rows_out
        stage[OWN, 0] = rows_out[OWN]
        copies = row_copies(total, stage, i)
        for copy in copies:
            copy.start()
        return copies

    tp_copy(y_acc, y_peer, 0).start()

    def use_grad(c):
        grad_sib(c).wait_recv()
        grad_fwd(c).wait_recv()
        grad_save(c).start()
        part = (_dot(grad[c, :, 0].reshape(all_rows, CHUNK), gate[c], 1, 1)
                + _dot(grad[c, :, 1].reshape(all_rows, CHUNK), up[c], 1, 1))
        dx_acc[...] += part.reshape(dx_acc.shape)

    def take_grad(c, carry):
        grad_far(c).wait_recv()
        grad_fwd(c).start()

        @pl.when(c > 0)
        def _():
            use_grad(c - 1)
        return carry

    lax.fori_loop(0, chunks, take_grad, 0)
    use_grad(chunks - 1)
    tp_copy(dx_acc, dx_peer, 1).start()
    copies = finish(xc, y_acc, y_peer, y_sum, y_stage, 0)
    copies += finish(dyc, dx_acc, dx_peer, dx_sum, dx_stage, 1)
    for copy in copies:
        copy.wait()
    last = [pltpu.make_async_copy(y_stage, y_out, in_sem.at[0]), pltpu.make_async_copy(dx_stage, dx_out, in_sem.at[1])]
    for copy in last:
        copy.start()

    for copy in token_copies:
        if copy is not None:
            copy.wait_send()
    for copy in keep_out:
        copy.wait()

    def drain(c, carry):
        for copy in (core_ab(c), core_g(c), link_ab(c), link_g(c), hid_far(c), hid_sib(c), hid_fwd(c),
                     grad_far(c), grad_sib(c), grad_fwd(c)):
            copy.wait_send()
        hid_save(c).wait()
        grad_save(c).wait()
        return carry

    lax.fori_loop(0, chunks, drain, 0)
    for copy in last:
        copy.wait()


def gradient_kernel(xc, dyc, hid, grad, y_stage, dx_stage, y_out, dx_out, dgate, dup, ddown, x_t):
    tp = lax.axis_index('tp')
    dp = lax.axis_index('dp')
    sib = dp + 1 - 2 * lax.rem(dp, 2)
    owner = {OWN: dp, FAR: lax.rem(dp + 2, SHARDS), SIB: sib, DIAG: lax.rem(sib + 2, SHARDS)}
    width = xc.shape[-1]
    all_rows = xc.shape[0] * xc.shape[1] * xc.shape[2]

    @pl.when(pl.program_id(0) == 0)
    def _():
        x_t[...] = xc[...].reshape(all_rows, width).T
        for stage, out in ((y_stage, y_out), (dx_stage, dx_out)):
            for p in range(SHARDS):
                at = pl.ds(pl.multiple_of(owner[p] * width, width), width)
                out[tp, :, at] = stage[p, 0]
                out[1 - tp, :, at] = stage[p, 1]

    dgate[...] = _dot(x_t[...], grad[0, :, 0].reshape(all_rows, CHUNK), 1, 0)
    dup[...] = _dot(x_t[...], grad[0, :, 1].reshape(all_rows, CHUNK), 1, 0)
    ddown[...] = _dot(hid[0].reshape(all_rows, CHUNK), dyc[...].reshape(all_rows, width), 0, 0)


def solution(mesh):
    def device_pass(x_rows, gate_blk, up_blk, down_blk, dy_rows):
        rows, model = x_rows.shape
        width, hidden = gate_blk.shape
        chunks = hidden // CHUNK
        half = rows // 2
        hbm = pl.BlockSpec(memory_space=pl.ANY)
        tok = (SHARDS, 2, half, width)
        sds = jax.ShapeDtypeStruct
        dma = pltpu.SemaphoreType.DMA
        xc, dyc, hid, grad, y_stage, dx_stage = pl.pallas_call(
            functools.partial(exchange_kernel, chunks),
            name='exchange',
            out_shape=(sds(tok, BF16), sds(tok, BF16), sds((chunks, SHARDS, rows, CHUNK), BF16),
                       sds((chunks, SHARDS, 2, rows, CHUNK), BF16), sds(tok, BF16), sds(tok, BF16)),
            in_specs=[hbm] * 5,
            out_specs=[hbm] * 6,
            scratch_shapes=[
                pltpu.VMEM((2, half, model), BF16), pltpu.VMEM((2, half, model), BF16),
                pltpu.VMEM(tok, BF16), pltpu.VMEM(tok, BF16),
                pltpu.VMEM((chunks, width, CHUNK), BF16), pltpu.VMEM((chunks, width, CHUNK), BF16),
                pltpu.VMEM((chunks, CHUNK, width), BF16),
                pltpu.VMEM((chunks, 2, 2, rows, CHUNK), F32), pltpu.VMEM((chunks, 2, 2, rows, CHUNK), F32),
                pltpu.VMEM((chunks, 2, 2, rows, CHUNK), F32),
                pltpu.VMEM((chunks, 2, rows, CHUNK), F32), pltpu.VMEM((chunks, 2, rows, CHUNK), F32),
                pltpu.VMEM((chunks, 2, rows, CHUNK), F32),
                pltpu.VMEM((chunks, 2, rows, CHUNK), F32), pltpu.VMEM((chunks, 2, rows, CHUNK), F32),
                pltpu.VMEM((chunks, rows, CHUNK), F32), pltpu.VMEM((chunks, rows, CHUNK), F32),
                pltpu.VMEM((chunks, SHARDS, rows, CHUNK), BF16), pltpu.VMEM((chunks, SHARDS, 2, rows, CHUNK), BF16),
                pltpu.VMEM(tok, F32), pltpu.VMEM(tok, F32),
                pltpu.VMEM((SHARDS, half, width), F32), pltpu.VMEM((SHARDS, half, width), F32),
                pltpu.VMEM((SHARDS, half, width), BF16), pltpu.VMEM((SHARDS, half, width), BF16),
                pltpu.VMEM(tok, BF16), pltpu.VMEM(tok, BF16),
                dma((4,)), dma((3, chunks)), dma((2, SHARDS)), dma((2, SHARDS)),
                dma((2, chunks)), dma((2, chunks)), dma((2, chunks)), dma((2, chunks)),
                dma((3, chunks)), dma((3, chunks)), dma((3, chunks)), dma((3, chunks)),
                dma((2,)), dma((2,)), dma((2, SHARDS, 2)), dma((2, SHARDS, 2)), dma((2 + 2 * chunks,)),
            ],
            compiler_params=pltpu.CompilerParams(collective_id=0, has_side_effects=True,
                                                 vmem_limit_bytes=60 * 1024 * 1024),
        )(x_rows.reshape(2, half, model), gate_blk, up_blk, down_blk, dy_rows.reshape(2, half, model))

        whole = lambda shape: pl.BlockSpec(shape, lambda c: (0,) * len(shape))
        y_rows, dx_rows, dw_gate, dw_up, dw_down = pl.pallas_call(
            gradient_kernel,
            name='gradients',
            grid=(chunks,),
            out_shape=(sds((2, half, model), BF16), sds((2, half, model), BF16), sds((width, hidden), F32),
                       sds((width, hidden), F32), sds((hidden, width), F32)),
            in_specs=[whole(tok), whole(tok),
                      pl.BlockSpec((1, SHARDS, rows, CHUNK), lambda c: (c, 0, 0, 0)),
                      pl.BlockSpec((1, SHARDS, 2, rows, CHUNK), lambda c: (c, 0, 0, 0, 0)),
                      whole(tok), whole(tok)],
            out_specs=[whole((2, half, model)), whole((2, half, model)),
                       pl.BlockSpec((width, CHUNK), lambda c: (0, c)), pl.BlockSpec((width, CHUNK), lambda c: (0, c)),
                       pl.BlockSpec((CHUNK, width), lambda c: (c, 0))],
            scratch_shapes=[pltpu.VMEM((width, all_rows := SHARDS * rows), BF16)],
            compiler_params=pltpu.CompilerParams(vmem_limit_bytes=48 * 1024 * 1024),
        )(xc, dyc, hid, grad, y_stage, dx_stage)
        return y_rows.reshape(rows, model), dx_rows.reshape(rows, model), dw_gate, dw_up, dw_down

    row_spec = P('dp', None)
    weight_spec = P('dp', 'tp')
    down_spec = P('tp', 'dp')
    return jax.shard_map(device_pass, mesh=mesh,
                         in_specs=(row_spec, weight_spec, weight_spec, down_spec, row_spec),
                         out_specs=(row_spec, row_spec, weight_spec, weight_spec, down_spec),
                         check_vma=False)
```

time: 244 us -> 102 us (0.42)
  waiting for transfers between devices: 119 us -> 0 us
  Pallas kernels: 0 us -> 95 us
  matrix products: 52.3 us -> 0 us
  local copies, waits for them, and re-layouts: 27.6 us -> 6.51 us
  blocking collectives: 17.4 us -> 0 us
  between operations: 14.2 us -> 0.65 us
  starting transfers between devices: 7.19 us -> 0 us
  other arithmetic: 5.88 us -> 0 us
    pallas_call x0 -> x2, Pallas kernels: none -> 95 us  [the longest x1 82 us: device_pass(): pl.pallas_call(functools.partial(exchange_kernel, chunks), name='exchange...]
    reduce_scatter x3 -> x0, waiting for transfers between devices: 64.9 us -> none  [the longest x1 28.6 us: device_pass(): lax.psum_scatter(gate_part, 'dp', scatter_dimension=0, tiled=True)]
    dot_general x9 -> x0, matrix products: 52.3 us -> none  [the longest x1 6.61 us: device_pass(): jnp.einsum('td,tf->df', x_cols, up_all, preferred_element_type=jnp.float32)]
    all_gather x3 -> x0, waiting for transfers between devices: 33.9 us -> none  [the longest x1 12.7 us: device_pass(): hidden_all = lax.all_gather(hidden, 'dp', axis=0, tiled=True)]
    unnamed x10 -> x12, local copies, waits for them, and re-layouts: 25.2 us -> 6.51 us
    all_to_all x2 -> x0, blocking collectives: 17.4 us -> none  [the longest x1 9.71 us: device_pass(): dy_cols = lax.all_to_all(dy_rows, 'dp', 1, 0, tiled=True)]
    psum x1 -> x0, waiting for transfers between devices: 15.7 us -> none  [device_pass(): lax.psum(out_part, 'tp')]
    all_to_all x2 -> x0, starting transfers between devices: 6.91 us -> none  [the longest x1 3.55 us: device_pass(): y_rows = lax.all_to_all(y_cols, 'dp', 0, 1, tiled=True)]
  transfers between devices with their start and end apart: 9 -> 0, of which waited for: 8 -> 0; matrix products, arithmetic and copies ran while one was open for 28% -> 0% of each run, Pallas kernels for 0% -> 0%
where the time goes in v1:
time: 102 us
  Pallas kernels  95 us (93%)
  local copies, waits for them, and re-layouts  6.51 us (6%)
    pallas_call x1, Pallas kernels, device_pass(): pl.pallas_call(functools.partial(exchange_kernel, chunks), name='exchange...  82 us
    pallas_call x1, Pallas kernels, device_pass(): pl.pallas_call(gradient_kernel, name='gradients', grid=(chunks,), out_sha...  13 us
    unnamed x12, local copies, waits for them, and re-layouts  6.51 us

profile of v1, /device:TPU:0, one launch (start us, length us, event | category | flops | bytes accessed | tf_op | source)
XLA Modules:
  0.0 102.2 jit_solution(15827614834626312588)
XLA Ops:
  0.6 82.0 %exchange.1 = (bf16[4,2,16,768]{3,2,1,0:T(8,128)(2,1)}, bf16[4,2,16,768]{3,2,1,0:T(8,128)(2,1)}, bf16[8,4,32,512]{3,2,1,0:T(8,128)(2,1)}, bf16[8,4,2,32,512]{4,3...) custom-call(bf16[2,16,3072]{2,1,0:T(8,128)(2,1)} %bitcast.4, ...), custom_call_target="tpu_custom_call" | custom-call | tf_op jit(solution)/shard_map/exchange/pallas_call | solution.py:329
  82.6 0.0 copy-start
  82.6 1.6 %copy-done = bf16[8,4,2,32,512]{4,3,2,1,0:T(8,128)(2,1)S(1)} copy-done((bf16[8,4,2,32,512]{4,3,2,1,0:T(8,128)(2,1)S(1)}, bf16[8,4,2,32,512]{4,3,2,1,0:T(8,128)(2,1)}, u32[]{:S(2)}) %copy-start) | copy-done | bytes 2097176
  84.2 0.0 copy-start.1
  84.2 1.2 %copy-done.1 = bf16[8,4,32,512]{3,2,1,0:T(8,128)(2,1)S(1)} copy-done((bf16[8,4,32,512]{3,2,1,0:T(8,128)(2,1)S(1)}, bf16[8,4,32,512]{3,2,1,0:T(8,128)(2,1)}, u32[]{:S(2)}) %copy-start.1) | copy-done | bytes 1048600
  85.5 0.0 copy-start.2
  85.5 0.9 copy-done.2
  86.4 0.0 copy-start.3
  86.4 0.9 copy-done.3
  87.3 0.0 copy-start.4
  87.3 0.9 copy-done.4
  88.2 0.0 copy-start.5
  88.2 0.9 copy-done.5
  89.2 13.0 %gradients.1 = (bf16[2,16,3072]{2,1,0:T(8,128)(2,1)}, bf16[2,16,3072]{2,1,0:T(8,128)(2,1)}, f32[768,4096]{1,0:T(8,128)}, f32[768,4096]{1,0:T(8,128)}, f32[4096,768]{1,0:T(8,128)}) custom-call(bf16[4,2,16,768]{3,2,1,0:T(8,128)(2,1)S(1)} %copy-done.2, bf16[4,2,16,768]{3,2,1,0:T(8,128)(2,1)S(1)} %copy-done.3, bf16[8,4,32,512]{3,2,1,0:T(8,128)(2,1)S(1)} %copy-done.1, ...), custom_call_target="tpu_custom_call" | custom-call | tf_op jit(solution)/shard_map/gradients/pallas_call | solution.py:362
Async XLA Ops:
  82.6 1.6 %copy-start = (bf16[8,4,2,32,512]{4,3,2,1,0:T(8,128)(2,1)S(1)}, bf16[8,4,2,32,512]{4,3,2,1,0:T(8,128)(2,1)}, u32[]{:S(2)}) copy-start(bf16[8,4,2,32,512]{4,3,2,1,0:T(8,128)(2,1)} %get-tuple-element.19.grad) | copy-start | bytes 6291460
  84.2 1.2 %copy-start.1 = (bf16[8,4,32,512]{3,2,1,0:T(8,128)(2,1)S(1)}, bf16[8,4,32,512]{3,2,1,0:T(8,128)(2,1)}, u32[]{:S(2)}) copy-start(bf16[8,4,32,512]{3,2,1,0:T(8,128)(2,1)} %get-tuple-element.18.hid) | copy-start | bytes 3145732
  85.5 0.9 copy-start.2
  86.4 0.9 copy-start.3
  87.3 0.9 copy-start.4
  88.2 0.9 copy-start.5

commit v2 on v1

v2 whole, which is shorter than its diff:
```python
import functools

import jax
import jax.numpy as jnp
from jax import lax
from jax.experimental import pallas as pl
from jax.experimental.pallas import tpu as pltpu
from jax.sharding import PartitionSpec as P

MESH = pl.DeviceIdType.MESH
F32 = jnp.float32
BF16 = jnp.bfloat16
CHUNK = 512
SHARDS = 4
OWN, SIB, FAR, DIAG = 0, 1, 2, 3


def _dot(lhs, rhs, lhs_dim, rhs_dim):
    return lax.dot_general(lhs, rhs, (((lhs_dim,), (rhs_dim,)), ((), ())), preferred_element_type=F32)


def exchange_kernel(chunks, x_hbm, gate_hbm, up_hbm, down_hbm, dy_hbm,
                    xc_out, dyc_out, hid_out, grad_out, y_out, dx_out,
                    x_own, dy_own, xc, dyc, gate, up, down,
                    ab_keep, ab_give, ab_got, g_keep, g_give, g_got, ab_recv, g_recv, hid, grad,
                    y_acc, dx_acc, y_peer, dx_peer, y_sum, dx_sum, y_stage, dx_stage,
                    in_sem, w_sem, tok_ss, tok_rs, core_ss, core_rs, link_ss, link_rs,
                    hid_ss, hid_rs, grad_ss, grad_rs, tp_ss, tp_rs, row_ss, row_rs, out_sem):
    tp = lax.axis_index('tp')
    dp = lax.axis_index('dp')
    sib = dp + 1 - 2 * lax.rem(dp, 2)
    far = lax.rem(dp + 2, SHARDS)
    diag = lax.rem(sib + 2, SHARDS)
    peers = {SIB: sib, FAR: far, DIAG: diag}
    width = xc.shape[-1]
    rows = x_own.shape[0] * x_own.shape[1]

    def remote(src, dst, ss, rs, **device):
        return pltpu.make_async_remote_copy(src_ref=src, dst_ref=dst, send_sem=ss, recv_sem=rs,
                                            device_id=device, device_id_type=MESH)

    def cols(i):
        return pl.ds(pl.multiple_of(i * width, width), width)

    def span(c):
        return pl.ds(pl.multiple_of(c * CHUNK, CHUNK), CHUNK)

    def load_gate(c):
        return pltpu.make_async_copy(gate_hbm.at[:, span(c)], gate.at[c], w_sem.at[0, c])

    def load_up(c):
        return pltpu.make_async_copy(up_hbm.at[:, span(c)], up.at[c], w_sem.at[1, c])

    def load_down(c):
        return pltpu.make_async_copy(down_hbm.at[span(c)], down.at[c], w_sem.at[2, c])

    tokens = ((x_hbm, x_own, xc, 0), (dy_hbm, dy_own, dyc, 1))
    stage_in = [pltpu.make_async_copy(h, v, in_sem.at[i]) for h, v, _, i in tokens]
    keep_in = [pltpu.make_async_copy(h.at[:, :, cols(dp)], s.at[OWN], in_sem.at[2 + i]) for h, _, s, i in tokens]
    for copy in stage_in + keep_in:
        copy.start()

    barrier = pltpu.get_barrier_semaphore()
    for p in (FAR, SIB, DIAG):
        pl.semaphore_signal(barrier, inc=1, device_id={'dp': peers[p]}, device_id_type=MESH)
        pl.semaphore_signal(barrier, inc=1, device_id={'dp': peers[p], 'tp': 1 - tp}, device_id_type=MESH)
    pl.semaphore_signal(barrier, inc=1, device_id={'tp': 1 - tp}, device_id_type=MESH)
    for copy in stage_in + keep_in:
        copy.wait()
    for c in range(chunks):
        load_gate(c).start()
        load_up(c).start()
    for c in range(chunks):
        load_down(c).start()
    pl.semaphore_wait(barrier, 2 * SHARDS - 1)

    def token(p, i):
        _, own, slots, _ = tokens[i]
        return remote(own.at[:, :, cols(peers[p])], slots.at[p], tok_ss.at[i, p], tok_rs.at[i, p], dp=peers[p])

    for i in (0, 1):
        for p in (SIB, FAR, DIAG):
            token(p, i).start()

    def core_ab(q, c):
        return remote(ab_give.at[q, c], ab_got.at[q, c], core_ss.at[q, 0, c], core_rs.at[q, 0, c], dp=sib)

    def core_g(q, c):
        return remote(g_give.at[q, c], g_got.at[q, c], core_ss.at[q, 1, c], core_rs.at[q, 1, c], dp=sib)

    def link_ab(c):
        return remote(ab_keep.at[0, c], ab_recv.at[c], link_ss.at[0, c], link_rs.at[0, c], dp=far)

    def link_g(c):
        return remote(g_keep.at[0, c], g_recv.at[c], link_ss.at[1, c], link_rs.at[1, c], dp=far)

    def send_ab(c):
        core_ab(0, c).wait_recv()
        ab_keep[0, c] += ab_got[0, c]
        link_ab(c).start()

    def send_g(c):
        core_g(0, c).wait_recv()
        g_keep[0, c] += g_got[0, c]
        link_g(c).start()

    def pair_rows(slots, q):
        return slots[2 * q:2 * q + 2].reshape(2 * rows, slots.shape[-1])

    def part_ab(q, c):
        tok = pair_rows(xc, q)
        for i, weight in enumerate((gate, up)):
            if q == 0:
                (load_gate, load_up)[i](c).wait()
            part = _dot(tok, weight[c], 1, 0)
            ab_keep[q, c, i] = part[:rows]
            ab_give[q, c, i] = part[rows:]
        core_ab(q, c).start()

    def part_g(q, c):
        if q == 0:
            load_down(c).wait()
        part = _dot(pair_rows(dyc, q), down[c], 1, 1)
        g_keep[q, c] = part[:rows]
        g_give[q, c] = part[rows:]
        core_g(q, c).start()

    def staggered(first, second, lower=0):
        def body(c, carry):
            first(c)

            @pl.when(c > 0)
            def _():
                second(c - 1)
            return carry

        lax.fori_loop(0, chunks, body, 0)
        second(chunks - 1)

    def each(body):
        lax.fori_loop(0, chunks, lambda c, carry: (body(c), carry)[1], 0)

    token(SIB, 0).wait_recv()
    staggered(functools.partial(part_ab, 0), send_ab)
    token(SIB, 1).wait_recv()
    staggered(functools.partial(part_g, 0), send_g)
    token(FAR, 0).wait_recv()
    token(DIAG, 0).wait_recv()
    each(functools.partial(part_ab, 1))
    token(FAR, 1).wait_recv()
    token(DIAG, 1).wait_recv()
    each(functools.partial(part_g, 1))

    keep_out = [pltpu.make_async_copy(xc, xc_out, out_sem.at[0]), pltpu.make_async_copy(dyc, dyc_out, out_sem.at[1])]
    for copy in keep_out:
        copy.start()

    def gathers(buf, ss, rs):
        def to_far(c):
            return remote(buf.at[c, FAR], buf.at[c, OWN], ss.at[0, c], rs.at[0, c], dp=far)

        def to_sib(c):
            return remote(buf.at[c, FAR], buf.at[c, DIAG], ss.at[1, c], rs.at[1, c], dp=sib)

        def forward(c):
            return remote(buf.at[c, OWN], buf.at[c, SIB], ss.at[2, c], rs.at[2, c], dp=sib)

        return to_far, to_sib, forward

    hid_far, hid_sib, hid_fwd = gathers(hid, hid_ss, hid_rs)
    grad_far, grad_sib, grad_fwd = gathers(grad, grad_ss, grad_rs)

    def hid_save(c):
        return pltpu.make_async_copy(hid.at[c], hid_out.at[c], out_sem.at[2 + c])

    def grad_save(c):
        return pltpu.make_async_copy(grad.at[c], grad_out.at[c], out_sem.at[2 + chunks + c])

    y_acc[...] = jnp.zeros_like(y_acc)
    dx_acc[...] = jnp.zeros_like(dx_acc)

    def add_y(q, c):
        part = _dot(hid[c, 2 * q:2 * q + 2].reshape(2 * rows, CHUNK), down[c], 1, 0)
        y_acc[q] += part.reshape(y_acc.shape[1:])

    def add_dx(q, c):
        part = (_dot(grad[c, 2 * q:2 * q + 2, 0].reshape(2 * rows, CHUNK), gate[c], 1, 1)
                + _dot(grad[c, 2 * q:2 * q + 2, 1].reshape(2 * rows, CHUNK), up[c], 1, 1))
        dx_acc[q] += part.reshape(dx_acc.shape[1:])

    def form_hidden(c):
        core_ab(1, c).wait_recv()
        link_ab(c).wait_recv()
        total = ab_keep[1, c] + ab_got[1, c] + ab_recv[c]
        ab_keep[1, c] = total
        a, b = total[0], total[1]
        hid[c, FAR] = (a * jax.nn.sigmoid(a) * b).astype(BF16)
        hid_far(c).start()
        hid_sib(c).start()

    def away_y(c):
        hid_sib(c).wait_recv()
        add_y(1, c)

    def form_grads(c):
        core_g(1, c).wait_recv()
        link_g(c).wait_recv()
        g = g_keep[1, c] + g_got[1, c] + g_recv[c]
        a, b = ab_keep[1, c, 0], ab_keep[1, c, 1]
        s = jax.nn.sigmoid(a)
        grad[c, FAR, 0] = (g * b * s * (1.0 + a * (1.0 - s))).astype(BF16)
        grad[c, FAR, 1] = (g * (a * s)).astype(BF16)
        grad_far(c).start()
        grad_sib(c).start()

    def away_dx(c):
        grad_sib(c).wait_recv()
        add_dx(1, c)

    results = ((xc, y_acc, y_peer, y_sum, y_stage), (dyc, dx_acc, dx_peer, dx_sum, dx_stage))

    def tp_copy(i, q):
        _, acc, peer, _, _ = results[i]
        return remote(acc.at[q, :, 1 - tp], peer.at[q], tp_ss.at[i, q], tp_rs.at[i, q], tp=1 - tp)

    def row_copies(i, q):
        _, _, _, total, stage = results[i]
        out = []
        for j in (0, 1):
            p = 2 * q + j
            for r in (0, 1):
                device = {} if p == OWN else {'dp': peers[p]}
                if r:
                    device['tp'] = 1 - tp
                if device:
                    out.append(remote(total.at[p], stage.at[p, r], row_ss.at[i, p, r], row_rs.at[i, p, r], **device))
        return out

    def finish(i, q):
        tok, acc, peer, total, stage = results[i]
        tp_copy(i, q).wait()
        total[2 * q:2 * q + 2] = (tok[2 * q:2 * q + 2, tp].astype(F32) + (acc[q, :, tp] + peer[q])).astype(BF16)
        if q == 0:
            stage[OWN, 0] = total[OWN]
        for copy in row_copies(i, q):
            copy.start()

    staggered(form_hidden, away_y)
    tp_copy(0, 1).start()
    staggered(form_grads, away_dx)
    tp_copy(1, 1).start()
    finish(0, 1)

    def take_hidden(c):
        hid_far(c).wait_recv()
        hid_fwd(c).start()

    def home_y(c):
        hid_fwd(c).wait_recv()
        hid_save(c).start()
        add_y(0, c)

    staggered(take_hidden, home_y)
    tp_copy(0, 0).start()
    finish(1, 1)

    def take_grad(c):
        grad_far(c).wait_recv()
        grad_fwd(c).start()

        @pl.when(c == chunks // 2)
        def _():
            finish(0, 0)

    def home_dx(c):
        grad_fwd(c).wait_recv()
        grad_save(c).start()
        add_dx(0, c)

    staggered(take_grad, home_dx)
    tp_copy(1, 0).start()
    finish(1, 0)
    for i in (0, 1):
        for q in (0, 1):
            for copy in row_copies(i, q):
                copy.wait()
    last = [pltpu.make_async_copy(y_stage, y_out, in_sem.at[0]), pltpu.make_async_copy(dx_stage, dx_out, in_sem.at[1])]
    for copy in last:
        copy.start()

    for i in (0, 1):
        for p in (SIB, FAR, DIAG):
            token(p, i).wait_send()
    for copy in keep_out:
        copy.wait()

    def drain(c):
        for copy in (core_ab(0, c), core_ab(1, c), core_g(0, c), core_g(1, c), link_ab(c), link_g(c),
                     hid_far(c), hid_sib(c), hid_fwd(c), grad_far(c), grad_sib(c), grad_fwd(c)):
            copy.wait_send()
        hid_save(c).wait()
        grad_save(c).wait()

    each(drain)
    for copy in last:
        copy.wait()


def gradient_kernel(xc, dyc, hid, grad, y_stage, dx_stage, y_out, dx_out, dgate, dup, ddown, x_t):
    tp = lax.axis_index('tp')
    dp = lax.axis_index('dp')
    sib = dp + 1 - 2 * lax.rem(dp, 2)
    owner = {OWN: dp, FAR: lax.rem(dp + 2, SHARDS), SIB: sib, DIAG: lax.rem(sib + 2, SHARDS)}
    width = xc.shape[-1]
    all_rows = xc.shape[0] * xc.shape[1] * xc.shape[2]

    @pl.when(pl.program_id(0) == 0)
    def _():
        x_t[...] = xc[...].reshape(all_rows, width).T
        for stage, out in ((y_stage, y_out), (dx_stage, dx_out)):
            for p in range(SHARDS):
                at = pl.ds(pl.multiple_of(owner[p] * width, width), width)
                out[tp, :, at] = stage[p, 0]
                out[1 - tp, :, at] = stage[p, 1]

    dgate[...] = _dot(x_t[...], grad[0, :, 0].reshape(all_rows, CHUNK), 1, 0)
    dup[...] = _dot(x_t[...], grad[0, :, 1].reshape(all_rows, CHUNK), 1, 0)
    ddown[...] = _dot(hid[0].reshape(all_rows, CHUNK), dyc[...].reshape(all_rows, width), 0, 0)


def solution(mesh):
    def device_pass(x_rows, gate_blk, up_blk, down_blk, dy_rows):
        rows, model = x_rows.shape
        width, hidden = gate_blk.shape
        chunks = hidden // CHUNK
        half = rows // 2
        hbm = pl.BlockSpec(memory_space=pl.ANY)
        tok = (SHARDS, 2, half, width)
        sds = jax.ShapeDtypeStruct
        dma = pltpu.SemaphoreType.DMA
        xc, dyc, hid, grad, y_stage, dx_stage = pl.pallas_call(
            functools.partial(exchange_kernel, chunks),
            name='exchange',
            out_shape=(sds(tok, BF16), sds(tok, BF16), sds((chunks, SHARDS, rows, CHUNK), BF16),
                       sds((chunks, SHARDS, 2, rows, CHUNK), BF16), sds(tok, BF16), sds(tok, BF16)),
            in_specs=[hbm] * 5,
            out_specs=[hbm] * 6,
            scratch_shapes=[
                pltpu.VMEM((2, half, model), BF16), pltpu.VMEM((2, half, model), BF16),
                pltpu.VMEM(tok, BF16), pltpu.VMEM(tok, BF16),
                pltpu.VMEM((chunks, width, CHUNK), BF16), pltpu.VMEM((chunks, width, CHUNK), BF16),
                pltpu.VMEM((chunks, CHUNK, width), BF16),
                pltpu.VMEM((2, chunks, 2, rows, CHUNK), F32), pltpu.VMEM((2, chunks, 2, rows, CHUNK), F32),
                pltpu.VMEM((2, chunks, 2, rows, CHUNK), F32),
                pltpu.VMEM((2, chunks, rows, CHUNK), F32), pltpu.VMEM((2, chunks, rows, CHUNK), F32),
                pltpu.VMEM((2, chunks, rows, CHUNK), F32),
                pltpu.VMEM((chunks, 2, rows, CHUNK), F32), pltpu.VMEM((chunks, rows, CHUNK), F32),
                pltpu.VMEM((chunks, SHARDS, rows, CHUNK), BF16), pltpu.VMEM((chunks, SHARDS, 2, rows, CHUNK), BF16),
                pltpu.VMEM((2, 2, 2, half, width), F32), pltpu.VMEM((2, 2, 2, half, width), F32),
                pltpu.VMEM((2, 2, half, width), F32), pltpu.VMEM((2, 2, half, width), F32),
                pltpu.VMEM((SHARDS, half, width), BF16), pltpu.VMEM((SHARDS, half, width), BF16),
                pltpu.VMEM(tok, BF16), pltpu.VMEM(tok, BF16),
                dma((4,)), dma((3, chunks)), dma((2, SHARDS)), dma((2, SHARDS)),
                dma((2, 2, chunks)), dma((2, 2, chunks)), dma((2, chunks)), dma((2, chunks)),
                dma((3, chunks)), dma((3, chunks)), dma((3, chunks)), dma((3, chunks)),
                dma((2, 2)), dma((2, 2)), dma((2, SHARDS, 2)), dma((2, SHARDS, 2)), dma((2 + 2 * chunks,)),
            ],
            compiler_params=pltpu.CompilerParams(collective_id=0, has_side_effects=True,
                                                 vmem_limit_bytes=60 * 1024 * 1024),
        )(x_rows.reshape(2, half, model), gate_blk, up_blk, down_blk, dy_rows.reshape(2, half, model))

        whole = lambda shape: pl.BlockSpec(shape, lambda c: (0,) * len(shape))
        y_rows, dx_rows, dw_gate, dw_up, dw_down = pl.pallas_call(
            gradient_kernel,
            name='gradients',
            grid=(chunks,),
            out_shape=(sds((2, half, model), BF16), sds((2, half, model), BF16), sds((width, hidden), F32),
                       sds((width, hidden), F32), sds((hidden, width), F32)),
            in_specs=[whole(tok), whole(tok),
                      pl.BlockSpec((1, SHARDS, rows, CHUNK), lambda c: (c, 0, 0, 0)),
                      pl.BlockSpec((1, SHARDS, 2, rows, CHUNK), lambda c: (c, 0, 0, 0, 0)),
                      whole(tok), whole(tok)],
            out_specs=[whole((2, half, model)), whole((2, half, model)),
                       pl.BlockSpec((width, CHUNK), lambda c: (0, c)), pl.BlockSpec((width, CHUNK), lambda c: (0, c)),
                       pl.BlockSpec((CHUNK, width), lambda c: (c, 0))],
            scratch_shapes=[pltpu.VMEM((width, all_rows := SHARDS * rows), BF16)],
            compiler_params=pltpu.CompilerParams(vmem_limit_bytes=62 * 1024 * 1024),
        )(xc, dyc, hid, grad, y_stage, dx_stage)
        return y_rows.reshape(rows, model), dx_rows.reshape(rows, model), dw_gate, dw_up, dw_down

    row_spec = P('dp', None)
    weight_spec = P('dp', 'tp')
    down_spec = P('tp', 'dp')
    return jax.shard_map(device_pass, mesh=mesh,
                         in_specs=(row_spec, weight_spec, weight_spec, down_spec, row_spec),
                         out_specs=(row_spec, row_spec, weight_spec, weight_spec, down_spec),
                         check_vma=False)
```

time: 102 us -> 89 us (0.87)
  Pallas kernels: 95 us -> 88.2 us
  local copies, waits for them, and re-layouts: 6.51 us -> 0 us
    pallas_call x1, Pallas kernels: 82 us -> 73.5 us  [device_pass(): pl.pallas_call(functools.partial(exchange_kernel, chunks), name='exchange...]
    unnamed x12 -> x0, local copies, waits for them, and re-layouts: 6.51 us -> none
    pallas_call x1, Pallas kernels: 13 us -> 14.7 us  [device_pass(): pl.pallas_call(gradient_kernel, name='gradients', grid=(chunks,), out_sha...]
where the time goes in v2:
time: 89 us; the launch traced here: 88.9 us
  Pallas kernels  88.2 us (99%)
    pallas_call x1, Pallas kernels, device_pass(): pl.pallas_call(functools.partial(exchange_kernel, chunks), name='exchange...  73.5 us
    pallas_call x1, Pallas kernels, device_pass(): pl.pallas_call(gradient_kernel, name='gradients', grid=(chunks,), out_sha...  14.7 us

profile of v2, /device:TPU:0, one launch (start us, length us, event | category | flops | bytes accessed | tf_op | source)
XLA Modules:
  0.0 88.9 jit_solution(744749018719622063)
XLA Ops:
  0.6 73.5 %exchange.1 = (bf16[4,2,16,768]{3,2,1,0:T(8,128)(2,1)}, bf16[4,2,16,768]{3,2,1,0:T(8,128)(2,1)}, bf16[8,4,32,512]{3,2,1,0:T(8,128)(2,1)}, bf16[8,4,2,32,512]{4,3...) custom-call(bf16[2,16,3072]{2,1,0:T(8,128)(2,1)} %bitcast.4, ...), custom_call_target="tpu_custom_call" | custom-call | tf_op jit(solution)/shard_map/exchange/pallas_call | solution.py:341
  74.2 14.7 %gradients.1 = (bf16[2,16,3072]{2,1,0:T(8,128)(2,1)}, bf16[2,16,3072]{2,1,0:T(8,128)(2,1)}, f32[768,4096]{1,0:T(8,128)}, f32[768,4096]{1,0:T(8,128)}, f32[4096,768]{1,0:T(8,128)}) custom-call(bf16[4,2,16,768]{3,2,1,0:T(8,128)(2,1)} %get-tuple-element.16.xc, bf16[4,2,16,768]{3,2,1,0:T(8,128)(2,1)} %get-tuple-element.17.dyc, ...), custom_call_target="tpu_custom_call" | custom-call | tf_op jit(solution)/shard_map/gradients/pallas_call | solution.py:373

commit v3 on v0

v3 whole, which is shorter than its diff:
```python
import jax
import jax.numpy as jnp
from jax import lax
from jax.experimental import pallas as pl
from jax.experimental.pallas import tpu as pltpu
from jax.sharding import PartitionSpec as P

MESH = pl.DeviceIdType.MESH
F32 = jnp.float32
BF16 = jnp.bfloat16
SHARDS = 4
CHUNK = 512
GROUP = 2 * CHUNK
TILE = 512
RING = 3
OWN, SIB, FAR, DIAG = 0, 1, 2, 3
(S_TOK, S_TOK_FWD, S_CORE_AB, S_CORE_G, S_LINK_AB, S_LINK_G, S_HID_FAR, S_HID_SIB, S_HID_FWD, S_GRAD_FAR, S_GRAD_SIB,
 S_GRAD_FWD, S_TP, S_ROW_HOME, S_ROW_AWAY, S_ROW_FWD, S_TAIL) = (0, 2, 4, 6, 8, 9, 10, 11, 12, 13, 14, 15, 16, 19, 20, 22, 23)
SENDS = 26


def _dot(lhs, rhs, lhs_dim, rhs_dim):
    return lax.dot_general(lhs, rhs, (((lhs_dim,), (rhs_dim,)), ((), ())), preferred_element_type=F32)


def exchange_kernel(x_own, gate_hbm, up_hbm, down_hbm, dy_own,
                    x_t, dyc, hid, grad, y_rows, dx_rows,
                    xc, gate_up, down,
                    ab_keep, ab_give, ab_got, g_keep, g_give, g_got, ab_recv, g_recv,
                    y_acc, dx_away, dx_home, y_peer, dx_peer, y_sum, dx_sum, y_stage, dx_stage, here_in, near_in,
                    send, gate_up_sem, down_sem, tok_rs, core_rs, away_rs, link_rs,
                    hid_rs, grad_rs, grad_sib_rs, tp_rs, home_rs, away_row_rs, tail_rs):
    tp = lax.axis_index('tp')
    dp = lax.axis_index('dp')
    sib = dp + 1 - 2 * lax.rem(dp, 2)
    far = lax.rem(dp + 2, SHARDS)
    diag = lax.rem(sib + 2, SHARDS)
    peers = {SIB: sib, FAR: far, DIAG: diag}
    half, width = xc.shape[-2:]
    groups = hid.shape[0]

    def remote(src, dst, ss, rs, **device):
        return pltpu.make_async_remote_copy(src_ref=src, dst_ref=dst, send_sem=send.at[ss], recv_sem=rs,
                                            device_id=device, device_id_type=MESH)

    def cols(i):
        return pl.ds(pl.multiple_of(i * width, width), width)

    def chunk_of(g, s):
        return pl.ds(pl.multiple_of(g * GROUP, GROUP) + s * CHUNK, CHUNK)

    def load_gate_up(g, s):
        sem = gate_up_sem.at[2 * g + s]
        return (pltpu.make_async_copy(gate_hbm.at[:, chunk_of(g, s)], gate_up.at[g, s, 0], sem),
                pltpu.make_async_copy(up_hbm.at[:, chunk_of(g, s)], gate_up.at[g, s, 1], sem))

    def load_down(g):
        return pltpu.make_async_copy(down_hbm.at[pl.ds(pl.multiple_of(g * GROUP, GROUP), GROUP)], down.at[g], down_sem.at[g])

    tokens = ((x_own, xc), (dy_own, dyc))
    barrier = pltpu.get_barrier_semaphore()
    for p in (FAR, SIB, DIAG):
        pl.semaphore_signal(barrier, inc=1, device_id={'dp': peers[p]}, device_id_type=MESH)
        pl.semaphore_signal(barrier, inc=1, device_id={'dp': peers[p], 'tp': 1 - tp}, device_id_type=MESH)
    pl.semaphore_signal(barrier, inc=1, device_id={'tp': 1 - tp}, device_id_type=MESH)
    for g in range(groups):
        for s in (0, 1):
            for copy in load_gate_up(g, s):
                copy.start()
    for g in range(groups):
        load_down(g).start()
    for own, slots in tokens:
        slots[:, OWN] = own[:, :, cols(dp)]
    pl.semaphore_wait(barrier, 2 * SHARDS - 1)

    def token(p, i):
        own, slots = tokens[i]
        if p == SIB:
            return remote(own.at[:, :, cols(sib)], slots.at[:, SIB], S_TOK + i, tok_rs.at[i, 0], dp=sib)
        return remote(own.at[tp, :, cols(peers[p])], slots.at[tp, p], S_TOK + i, tok_rs.at[i, 1], dp=peers[p])

    def token_fwd(i):
        part = tokens[i][1].at[tp, 2:4]
        return remote(part, part, S_TOK_FWD + i, tok_rs.at[i, 2], tp=1 - tp)

    def tokens_far(i):
        part = tokens[i][1].at[tp, 2:4]
        return remote(part, part, S_TOK + i, tok_rs.at[i, 1], dp=far)

    for i in (0, 1):
        for p in (SIB, FAR, DIAG):
            token(p, i).start()

    def core_ab(q, c):
        rs = core_rs.at[0, c] if q == 0 else away_rs.at[0]
        return remote(ab_give.at[q, c], ab_got.at[q, c], S_CORE_AB + q, rs, dp=sib)

    def core_g(q, c):
        rs = core_rs.at[1, c] if q == 0 else away_rs.at[1]
        return remote(g_give.at[q, c], g_got.at[q, c], S_CORE_G + q, rs, dp=sib)

    def link_ab(c):
        return remote(ab_keep.at[0, c], ab_recv.at[c], S_LINK_AB, link_rs.at[0, c], dp=far)

    def link_g(c):
        return remote(g_keep.at[0, c], g_recv.at[c], S_LINK_G, link_rs.at[1, c], dp=far)

    def send_ab(c):
        core_ab(0, c).wait_recv()
        ab_keep[0, c] += ab_got[0, c]
        link_ab(c).start()

    def send_g(c):
        core_g(0, c).wait_recv()
        g_keep[0, c] += g_got[0, c]
        link_g(c).start()

    def pair_rows(slots, q):
        return slots[:, 2 * q:2 * q + 2].reshape(4 * half, slots.shape[-1])

    def split(part):
        part = part.reshape(2, 2, half, part.shape[-1])
        return part[:, 0], part[:, 1]

    def part_ab(q, g, s):
        c = 2 * g + s
        if q == 0:
            pltpu.make_async_copy(gate_up.at[g, s], gate_up.at[g, s], gate_up_sem.at[c]).wait()
        tok = pair_rows(xc, q)
        for i in (0, 1):
            ab_keep[q, c, i], ab_give[q, c, i] = split(_dot(tok, gate_up[g, s, i], 1, 0))
        core_ab(q, c).start()

    def part_g(q, g, s):
        c = 2 * g + s
        if q == 0 and s == 0:
            load_down(g).wait()
        g_keep[q, c], g_give[q, c] = split(_dot(pair_rows(dyc, q), down[g, s * CHUNK:(s + 1) * CHUNK], 1, 1))
        core_g(q, c).start()

    def each(body):
        lax.fori_loop(0, groups, lambda g, carry: (body(g), carry)[1], 0)

    def behind(first, second):
        def body(g):
            first(g)

            @pl.when(g > 0)
            def _():
                second(g - 1)

        each(body)
        second(groups - 1)

    def home_parts(part, send_on):
        def body(g):
            part(0, g, 0)

            @pl.when(g > 0)
            def _():
                send_on(2 * g - 1)
            part(0, g, 1)
            send_on(2 * g)

        each(body)
        send_on(2 * groups - 1)

    def away_parts(part):
        each(lambda g: (part(1, g, 0), part(1, g, 1)))

    token(SIB, 0).wait_recv()
    home_parts(part_ab, send_ab)
    for i in (0, 1):
        tokens_far(i).wait_recv()
        token_fwd(i).start()
    token(SIB, 1).wait_recv()
    home_parts(part_g, send_g)
    token_fwd(0).wait_recv()
    away_parts(part_ab)
    token_fwd(1).wait_recv()
    away_parts(part_g)
    x_t[...] = xc[...].reshape(2 * SHARDS * half, width).T

    def hid_far(g):
        return remote(hid.at[g, :, FAR], hid.at[g, :, OWN], S_HID_FAR, hid_rs.at[0, g], dp=far)

    def hid_sib(g):
        return remote(hid.at[g, :, FAR], hid.at[g, :, DIAG], S_HID_SIB, hid_rs.at[1, g], dp=sib)

    def hid_fwd(g):
        return remote(hid.at[g, :, OWN], hid.at[g, :, SIB], S_HID_FWD, hid_rs.at[2, g], dp=sib)

    def grad_far(g, h):
        return remote(grad.at[g, h, FAR], grad.at[g, h, OWN], S_GRAD_FAR, grad_rs.at[0, h, g], dp=far)

    def grad_sib(g):
        return remote(grad.at[g, :, FAR], grad.at[g, :, DIAG], S_GRAD_SIB, grad_sib_rs, dp=sib)

    def grad_fwd(g, h):
        return remote(grad.at[g, h, OWN], grad.at[g, h, SIB], S_GRAD_FWD, grad_rs.at[1, h, g], dp=sib)

    y_acc[...] = jnp.zeros_like(y_acc)
    dx_away[...] = jnp.zeros_like(dx_away)
    dx_home[...] = jnp.zeros_like(dx_home)

    def add_y(q, g):
        part = _dot(hid[g, :, 2 * q:2 * q + 2].reshape(4 * half, GROUP), down[g], 1, 0)
        y_acc[q] += part.reshape(y_acc.shape[1:])

    def dx_part(take, count, g):
        part = None
        for s in (0, 1):
            for i in (0, 1):
                lhs = take(i, s * CHUNK).reshape(count, CHUNK)
                term = _dot(lhs, gate_up[g, s, i], 1, 1)
                part = term if part is None else part + term
        return part

    def add_dx_away(g):
        part = dx_part(lambda i, at: grad[g, :, 2:4, i, :, at:at + CHUNK], 4 * half, g)
        dx_away[...] += part.reshape(dx_away.shape)

    def add_dx_home(g, h):
        part = dx_part(lambda i, at: grad[g, h, 0:2, i, :, at:at + CHUNK], 2 * half, g)
        dx_home[h] += part.reshape(dx_home.shape[1:])

    def form_hidden(g):
        for s in (0, 1):
            c = 2 * g + s
            link_ab(c).wait_recv()
            total = ab_keep[1, c] + ab_got[1, c] + ab_recv[c]
            ab_keep[1, c] = total
            a, b = total[0], total[1]
            hid[g, :, FAR, :, s * CHUNK:(s + 1) * CHUNK] = (a * jax.nn.sigmoid(a) * b).astype(BF16)
        hid_far(g).start()
        hid_sib(g).start()

    def away_y(g):
        hid_sib(g).wait_recv()
        add_y(1, g)

    def form_grads(g):
        for s in (0, 1):
            c = 2 * g + s
            link_g(c).wait_recv()
            v = g_keep[1, c] + g_got[1, c] + g_recv[c]
            a, b = ab_keep[1, c, 0], ab_keep[1, c, 1]
            sig = jax.nn.sigmoid(a)
            grad[g, :, FAR, 0, :, s * CHUNK:(s + 1) * CHUNK] = (v * b * sig * (1.0 + a * (1.0 - sig))).astype(BF16)
            grad[g, :, FAR, 1, :, s * CHUNK:(s + 1) * CHUNK] = (v * (a * sig)).astype(BF16)
        grad_far(g, 0).start()
        grad_sib(g).start()

    def tp_copy(acc, peer, k):
        return remote(acc.at[1 - tp], peer, S_TP + k, tp_rs.at[k], tp=1 - tp)

    y_tp = [tp_copy(y_acc.at[q], y_peer.at[q], q) for q in (0, 1)]
    dx_tp = tp_copy(dx_away, dx_peer, 2)

    def row_home(p, r):
        device = {} if p == OWN else {'dp': sib}
        if r:
            device['tp'] = 1 - tp
        return remote(y_sum.at[p], y_stage.at[p, r], S_ROW_HOME, home_rs.at[2 if p == OWN else r], **device)

    home_rows = ((OWN, 1), (SIB, 0), (SIB, 1))

    def y_away(p):
        return remote(y_sum.at[p], y_stage.at[p, 0], S_ROW_AWAY, away_row_rs.at[0], dp=peers[p])

    def y_away_all():
        return remote(y_sum.at[2:4], y_stage.at[2:4, 0], S_ROW_AWAY, away_row_rs.at[0], dp=far)

    def y_away_fwd():
        return remote(y_stage.at[2:4, 0], y_stage.at[2:4, 1], S_ROW_FWD, away_row_rs.at[1], tp=1 - tp)

    def dx_row(p, r):
        device = {'dp': peers[p]}
        if r:
            device['tp'] = 1 - tp
        return remote(dx_sum.at[p - 2], dx_stage.at[r, p - 2], S_ROW_AWAY + 1, away_row_rs.at[2 + r], **device)

    def dx_row_all(r):
        return remote(dx_sum, dx_stage.at[r], S_ROW_AWAY + 1, away_row_rs.at[2 + r], dp=far)

    def finish_y(q):
        y_tp[q].wait()
        y_sum[2 * q:2 * q + 2] = (xc[tp, 2 * q:2 * q + 2].astype(F32) + (y_acc[q, tp] + y_peer[q])).astype(BF16)
        if q == 0:
            y_stage[OWN, 0] = y_sum[OWN]
            for p, r in home_rows:
                row_home(p, r).start()
        else:
            for p in (FAR, DIAG):
                y_away(p).start()

    def tail(h):
        return (remote(dx_home.at[h, 0], here_in.at[h], S_TAIL, tail_rs.at[h, 0], tp=1 - tp),
                remote(dx_home.at[h, 1], near_in.at[h, 1], S_TAIL + 1, tail_rs.at[h, 1], dp=sib, tp=1 - tp),
                remote(dx_home.at[h, 1], near_in.at[h, 0], S_TAIL + 2, tail_rs.at[h, 2], dp=sib))

    def finish_dx_home(h):
        for copy in tail(h):
            copy.wait_recv()
        dx_rows[h, :, cols(dp)] = (dyc[h, OWN].astype(F32) + (dx_home[h, 0] + here_in[h])).astype(BF16)
        dx_rows[h, :, cols(sib)] = (dy_own[h, :, cols(sib)].astype(F32) + (near_in[h, 0] + near_in[h, 1])).astype(BF16)

    remote(ab_give.at[1], ab_got.at[1], S_CORE_AB + 1, away_rs.at[0], dp=sib).wait()
    behind(form_hidden, away_y)
    y_tp[1].start()
    remote(g_give.at[1], g_got.at[1], S_CORE_G + 1, away_rs.at[1], dp=sib).wait()
    each(form_grads)
    finish_y(1)
    each(lambda g: grad_far(g, 1).start())

    def take_hidden(g):
        hid_far(g).wait_recv()
        hid_fwd(g).start()

    def home_y(g):
        hid_fwd(g).wait_recv()
        add_y(0, g)
        add_dx_away(g)

    remote(grad.at[:, :, FAR], grad.at[:, :, DIAG], S_GRAD_SIB, grad_sib_rs, dp=sib).wait()
    behind(take_hidden, home_y)
    y_tp[0].start()
    dx_tp.start()

    def take_grad(h):
        def body(g):
            grad_far(g, h).wait_recv()
            grad_fwd(g, h).start()
        return body

    def home_dx(h):
        def body(g):
            grad_fwd(g, h).wait_recv()
            add_dx_home(g, h)
        return body

    behind(take_grad(0), home_dx(0))
    for copy in tail(0):
        copy.start()
    finish_y(0)
    y_away_all().wait_recv()
    y_away_fwd().start()
    dx_tp.wait()
    dx_sum[...] = (dyc[tp, 2:4].astype(F32) + (dx_away[tp] + dx_peer[...])).astype(BF16)

    each_home = home_dx(1)

    def last_grads(g):
        take_grad(1)(g)

        @pl.when(g == groups - 1)
        def _():
            for p in (FAR, DIAG):
                for r in (1, 0):
                    dx_row(p, r).start()

    behind(last_grads, each_home)
    for copy in tail(1):
        copy.start()

    finish_dx_home(0)
    for p, r in home_rows:
        row_home(p, r).wait_recv()
    y_away_fwd().wait_recv()
    owner = {OWN: dp, SIB: sib, FAR: far, DIAG: diag}
    for p in range(SHARDS):
        y_rows[tp, :, cols(owner[p])] = y_stage[p, 0]
        y_rows[1 - tp, :, cols(owner[p])] = y_stage[p, 1]

    for i in (0, 1):
        slots = tokens[i][1]
        remote(slots.at[:, 0:2], slots.at[:, 0:2], S_TOK + i, tok_rs.at[i, 0], dp=sib).wait_send()
        token_fwd(i).wait_send()
    remote(ab_give.at[0], ab_got.at[0], S_CORE_AB, core_rs.at[0, 0], dp=sib).wait_send()
    remote(g_give.at[0], g_got.at[0], S_CORE_G, core_rs.at[0, 0], dp=sib).wait_send()
    remote(ab_keep.at[0], ab_recv, S_LINK_AB, link_rs.at[0, 0], dp=far).wait_send()
    remote(g_keep.at[0], g_recv, S_LINK_G, link_rs.at[0, 0], dp=far).wait_send()
    for kind in (S_HID_FAR, S_HID_SIB, S_HID_FWD):
        remote(hid.at[:, :, OWN], hid.at[:, :, SIB], kind, hid_rs.at[0, 0], dp=sib).wait_send()
    for kind in (S_GRAD_FAR, S_GRAD_FWD):
        remote(grad.at[:, :, OWN], grad.at[:, :, SIB], kind, grad_sib_rs, dp=sib).wait_send()
    remote(y_sum.at[0:3], y_sum.at[0:3], S_ROW_HOME, home_rs.at[0], dp=sib).wait_send()
    y_away_all().wait_send()
    y_away_fwd().wait_send()
    remote(dx_stage, dx_stage, S_ROW_AWAY + 1, away_row_rs.at[2], dp=far).wait_send()

    for r in (0, 1):
        dx_row_all(r).wait_recv()
    for p in (FAR, DIAG):
        dx_rows[tp, :, cols(owner[p])] = dx_stage[0, p - 2]
        dx_rows[1 - tp, :, cols(owner[p])] = dx_stage[1, p - 2]
    finish_dx_home(1)
    for k in range(3):
        remote(dx_home.at[:, 0], here_in, S_TAIL + k, tail_rs.at[0, 0], dp=sib).wait_send()


def gradient_kernel(x_t, dyc, hid, grad, y_rows, dx_rows, y_out, dx_out, dgate_out, dup_out, ddown_out,
                    dgate, dup, ddown, row_sem, tile_sem):
    groups = hid.shape[0]
    tokens = x_t.shape[1]
    width = dyc.shape[-1]
    per_group = GROUP // TILE
    rows_out = [pltpu.make_async_copy(y_rows, y_out, row_sem.at[0]), pltpu.make_async_copy(dx_rows, dx_out, row_sem.at[1])]

    def write(n, slot, k):
        at = pl.ds(pl.multiple_of(n * TILE, TILE), TILE)
        out = ddown_out.at[at] if k == 2 else (dgate_out, dup_out)[k].at[:, at]
        return pltpu.make_async_copy((dgate, dup, ddown)[k].at[slot], out, tile_sem.at[k, slot])

    def body(g, carry):
        for s in range(per_group):
            n = g * per_group + s
            slot = lax.rem(n, RING)

            def take(k):
                @pl.when(n >= RING)
                def _():
                    write(n - RING, slot, k).wait()

            at = slice(s * TILE, (s + 1) * TILE)
            for k, buf in enumerate((dgate, dup)):
                take(k)
                buf[slot] = _dot(x_t[...], grad[g, :, :, k, :, at].reshape(tokens, TILE), 1, 0)
                write(n, slot, k).start()
            take(2)
            ddown[slot] = _dot(hid[g, :, :, :, at].reshape(tokens, TILE), dyc[...].reshape(tokens, width), 0, 0)
            write(n, slot, 2).start()
        return carry

    lax.fori_loop(0, groups, body, 0)
    for copy in rows_out:
        copy.start()
    for n in range(groups * per_group - RING, groups * per_group):
        for k in range(3):
            write(n, n % RING, k).wait()
    for copy in rows_out:
        copy.wait()


def solution(mesh):
    def device_pass(x_rows, gate_blk, up_blk, down_blk, dy_rows):
        rows, model = x_rows.shape
        width, hidden = gate_blk.shape
        chunks, groups = hidden // CHUNK, hidden // GROUP
        half = rows // 2
        tokens = SHARDS * rows
        hbm = pl.BlockSpec(memory_space=pl.ANY)
        vmem = pl.BlockSpec(memory_space=pltpu.VMEM)
        sds = jax.ShapeDtypeStruct
        dma = pltpu.SemaphoreType.DMA
        tok = (2, SHARDS, half, width)
        block = (2, half, width)
        own = (2, half, model)
        x_t, dyc, hid, grad, y_own, dx_own = pl.pallas_call(
            exchange_kernel,
            name='exchange',
            out_shape=(sds((width, tokens), BF16), sds(tok, BF16), sds((groups, 2, SHARDS, half, GROUP), BF16),
                       sds((groups, 2, SHARDS, 2, half, GROUP), BF16), sds(own, BF16), sds(own, BF16)),
            in_specs=[vmem, hbm, hbm, hbm, vmem],
            out_specs=[vmem] * 6,
            scratch_shapes=[
                pltpu.VMEM(tok, BF16),
                pltpu.VMEM((groups, 2, 2, width, CHUNK), BF16), pltpu.VMEM((groups, GROUP, width), BF16),
                pltpu.VMEM((2, chunks, 2, 2, half, CHUNK), F32), pltpu.VMEM((2, chunks, 2, 2, half, CHUNK), F32),
                pltpu.VMEM((2, chunks, 2, 2, half, CHUNK), F32),
                pltpu.VMEM((2, chunks, 2, half, CHUNK), F32), pltpu.VMEM((2, chunks, 2, half, CHUNK), F32),
                pltpu.VMEM((2, chunks, 2, half, CHUNK), F32),
                pltpu.VMEM((chunks, 2, 2, half, CHUNK), F32), pltpu.VMEM((chunks, 2, half, CHUNK), F32),
                pltpu.VMEM((2, 2) + block, F32), pltpu.VMEM((2,) + block, F32), pltpu.VMEM((2,) + block, F32),
                pltpu.VMEM((2,) + block, F32), pltpu.VMEM(block, F32),
                pltpu.VMEM((SHARDS, half, width), BF16), pltpu.VMEM(block, BF16),
                pltpu.VMEM((SHARDS, 2, half, width), BF16), pltpu.VMEM((2,) + block, BF16),
                pltpu.VMEM(block, F32), pltpu.VMEM((2,) + block, F32),
                dma((SENDS,)), dma((chunks,)), dma((groups,)), dma((2, 3)), dma((2, chunks)), dma((2,)),
                dma((2, chunks)), dma((3, groups)), dma((2, 2, groups)), dma(()), dma((3,)), dma((3,)), dma((4,)), dma((2, 3)),
            ],
            compiler_params=pltpu.CompilerParams(collective_id=0, has_side_effects=True,
                                                 vmem_limit_bytes=44 * 1024 * 1024),
        )(x_rows.reshape(own), gate_blk, up_blk, down_blk, dy_rows.reshape(own))

        y_new, dx_new, dw_gate, dw_up, dw_down = pl.pallas_call(
            gradient_kernel,
            name='gradients',
            out_shape=(sds(own, BF16), sds(own, BF16), sds((width, hidden), F32), sds((width, hidden), F32),
                       sds((hidden, width), F32)),
            in_specs=[vmem] * 6,
            out_specs=[hbm] * 5,
            scratch_shapes=[pltpu.VMEM((RING, width, TILE), F32), pltpu.VMEM((RING, width, TILE), F32),
                            pltpu.VMEM((RING, TILE, width), F32), dma((2,)), dma((3, RING))],
            compiler_params=pltpu.CompilerParams(vmem_limit_bytes=44 * 1024 * 1024),
        )(x_t, dyc, hid, grad, y_own, dx_own)
        return y_new.reshape(rows, model), dx_new.reshape(rows, model), dw_gate, dw_up, dw_down

    row_spec = P('dp', None)
    weight_spec = P('dp', 'tp')
    down_spec = P('tp', 'dp')
    return jax.shard_map(device_pass, mesh=mesh,
                         in_specs=(row_spec, weight_spec, weight_spec, down_spec, row_spec),
                         out_specs=(row_spec, row_spec, weight_spec, weight_spec, down_spec),
                         check_vma=False)
```

time: 244 us -> 82.9 us (0.34)
  waiting for transfers between devices: 119 us -> 0 us
  Pallas kernels: 0 us -> 80.3 us
  matrix products: 52.3 us -> 0 us
  local copies, waits for them, and re-layouts: 27.6 us -> 1.85 us
  blocking collectives: 17.4 us -> 0 us
  between operations: 14.2 us -> 0.65 us
  starting transfers between devices: 7.19 us -> 0 us
  other arithmetic: 5.88 us -> 0 us
    pallas_call x0 -> x2, Pallas kernels: none -> 80.3 us  [the longest x1 67.6 us: device_pass(): pl.pallas_call(exchange_kernel, name='exchange', out_shape=(sds((width, t...]
    reduce_scatter x3 -> x0, waiting for transfers between devices: 64.9 us -> none  [the longest x1 28.6 us: device_pass(): lax.psum_scatter(gate_part, 'dp', scatter_dimension=0, tiled=True)]
    dot_general x9 -> x0, matrix products: 52.3 us -> none  [the longest x1 6.61 us: device_pass(): jnp.einsum('td,tf->df', x_cols, up_all, preferred_element_type=jnp.float32)]
    all_gather x3 -> x0, waiting for transfers between devices: 33.9 us -> none  [the longest x1 12.7 us: device_pass(): hidden_all = lax.all_gather(hidden, 'dp', axis=0, tiled=True)]
    unnamed x10 -> x4, local copies, waits for them, and re-layouts: 25.2 us -> 1.85 us
    all_to_all x2 -> x0, blocking collectives: 17.4 us -> none  [the longest x1 9.71 us: device_pass(): dy_cols = lax.all_to_all(dy_rows, 'dp', 1, 0, tiled=True)]
    psum x1 -> x0, waiting for transfers between devices: 15.7 us -> none  [device_pass(): lax.psum(out_part, 'tp')]
    all_to_all x2 -> x0, starting transfers between devices: 6.91 us -> none  [the longest x1 3.55 us: device_pass(): y_rows = lax.all_to_all(y_cols, 'dp', 0, 1, tiled=True)]
  transfers between devices with their start and end apart: 9 -> 0, of which waited for: 8 -> 0; matrix products, arithmetic and copies ran while one was open for 28% -> 0% of each run, Pallas kernels for 0% -> 0%
where the time goes in v3:
time: 82.9 us; the launch traced here: 82.8 us
  Pallas kernels  80.3 us (97%)
  local copies, waits for them, and re-layouts  1.85 us (2%)
    pallas_call x1, Pallas kernels, device_pass(): pl.pallas_call(exchange_kernel, name='exchange', out_shape=(sds((width, t...  67.6 us
    pallas_call x1, Pallas kernels, device_pass(): pl.pallas_call(gradient_kernel, name='gradients', out_shape=(sds(own, BF1...  12.7 us
    unnamed x4, local copies, waits for them, and re-layouts  1.85 us

profile of v3, /device:TPU:0, one launch (start us, length us, event | category | flops | bytes accessed | tf_op | source)
XLA Modules:
  0.0 82.8 jit_solution(1310257836855933675)
XLA Ops:
  0.6 0.0 copy-start
  0.6 0.9 %copy-done = bf16[32,3072]{1,0:T(8,128)(2,1)S(1)} copy-done((bf16[32,3072]{1,0:T(8,128)(2,1)S(1)}, bf16[32,3072]{1,0:T(8,128)(2,1)}, u32[]{:S(2)}) %copy-start) | copy-done | bytes 196632
  1.6 0.0 copy-start.1
  1.6 0.9 %copy-done.1 = bf16[32,3072]{1,0:T(8,128)(2,1)S(1)} copy-done((bf16[32,3072]{1,0:T(8,128)(2,1)S(1)}, bf16[32,3072]{1,0:T(8,128)(2,1)}, u32[]{:S(2)}) %copy-start.1) | copy-done | bytes 196632
  2.5 67.6 %exchange.1 = (bf16[768,128]{1,0:T(8,128)(2,1)S(1)}, bf16[2,4,16,768]{3,2,1,0:T(8,128)(2,1)S(1)}, bf16[4,2,4,16,1024]{4,3,2,1,0:T(8,128)(2,1)S(1)}, bf16[4,2,4,2...) custom-call(bf16[2,16,3072]{2,1,0:T(8,128)(2,1)S(1)} %bitcast.4, ...), custom_call_target="tpu_custom_call" | custom-call | tf_op jit(solution)/shard_map/exchange/pallas_call | solution.py:459
  70.0 12.7 %gradients.1 = (bf16[2,16,3072]{2,1,0:T(8,128)(2,1)}, bf16[2,16,3072]{2,1,0:T(8,128)(2,1)}, f32[768,4096]{1,0:T(8,128)}, f32[768,4096]{1,0:T(8,128)}, f32[4096,768]{1,0:T(8,128)}) custom-call(bf16[768,128]{1,0:T(8,128)(2,1)S(1)} %get-tuple-element.16.x_t, bf16[2,4,16,768]{3,2,1,0:T(8,128)(2,1)S(1)} %get-tuple-element.17.dyc, ...), custom_call_target="tpu_custom_call" | custom-call | tf_op jit(solution)/shard_map/gradients/pallas_call | solution.py:486
Async XLA Ops:
  0.6 0.9 %copy-start = (bf16[32,3072]{1,0:T(8,128)(2,1)S(1)}, bf16[32,3072]{1,0:T(8,128)(2,1)}, u32[]{:S(2)}) copy-start(bf16[32,3072]{1,0:T(8,128)(2,1)} %param.5) | copy-start | bytes 589828
  1.6 0.9 %copy-start.1 = (bf16[32,3072]{1,0:T(8,128)(2,1)S(1)}, bf16[32,3072]{1,0:T(8,128)(2,1)}, u32[]{:S(2)}) copy-start(bf16[32,3072]{1,0:T(8,128)(2,1)} %param.9) | copy-start | bytes 589828

commit v4 on v3

--- a/solution.py
+++ b/solution.py
@@ -23,7 +23,7 @@
     return lax.dot_general(lhs, rhs, (((lhs_dim,), (rhs_dim,)), ((), ())), preferred_element_type=F32)
 
 
-def exchange_kernel(x_own, gate_hbm, up_hbm, down_hbm, dy_own,
+def exchange_kernel(token_rows, gate_hbm, up_hbm, down_hbm,
                     x_t, dyc, hid, grad, y_rows, dx_rows,
                     xc, gate_up, down,
                     ab_keep, ab_give, ab_got, g_keep, g_give, g_got, ab_recv, g_recv,
@@ -57,7 +57,8 @@
     def load_down(g):
         return pltpu.make_async_copy(down_hbm.at[pl.ds(pl.multiple_of(g * GROUP, GROUP), GROUP)], down.at[g], down_sem.at[g])
 
-    tokens = ((x_own, xc), (dy_own, dyc))
+    tokens = ((token_rows.at[0], xc), (token_rows.at[1], dyc))
+    dy_own = token_rows.at[1]
     barrier = pltpu.get_barrier_semaphore()
     for p in (FAR, SIB, DIAG):
         pl.semaphore_signal(barrier, inc=1, device_id={'dp': peers[p]}, device_id_type=MESH)
@@ -91,24 +92,24 @@
         for p in (SIB, FAR, DIAG):
             token(p, i).start()
 
-    def core_ab(q, c):
-        rs = core_rs.at[0, c] if q == 0 else away_rs.at[0]
-        return remote(ab_give.at[q, c], ab_got.at[q, c], S_CORE_AB + q, rs, dp=sib)
+    def core_ab(q, c, i):
+        rs = core_rs.at[i, c] if q == 0 else away_rs.at[0]
+        return remote(ab_give.at[q, c, i], ab_got.at[q, c, i], S_CORE_AB + q, rs, dp=sib)
 
     def core_g(q, c):
-        rs = core_rs.at[1, c] if q == 0 else away_rs.at[1]
+        rs = core_rs.at[2, c] if q == 0 else away_rs.at[1]
         return remote(g_give.at[q, c], g_got.at[q, c], S_CORE_G + q, rs, dp=sib)
 
-    def link_ab(c):
-        return remote(ab_keep.at[0, c], ab_recv.at[c], S_LINK_AB, link_rs.at[0, c], dp=far)
+    def link_ab(c, i):
+        return remote(ab_keep.at[0, c, i], ab_recv.at[c, i], S_LINK_AB, link_rs.at[i, c], dp=far)
 
     def link_g(c):
-        return remote(g_keep.at[0, c], g_recv.at[c], S_LINK_G, link_rs.at[1, c], dp=far)
-
-    def send_ab(c):
-        core_ab(0, c).wait_recv()
-        ab_keep[0, c] += ab_got[0, c]
-        link_ab(c).start()
+        return remote(g_keep.at[0, c], g_recv.at[c], S_LINK_G, link_rs.at[2, c], dp=far)
+
+    def send_ab(c, i):
+        core_ab(0, c, i).wait_recv()
+        ab_keep[0, c, i] += ab_got[0, c, i]
+        link_ab(c, i).start()
 
     def send_g(c):
         core_g(0, c).wait_recv()
@@ -122,14 +123,12 @@
         part = part.reshape(2, 2, half, part.shape[-1])
         return part[:, 0], part[:, 1]
 
-    def part_ab(q, g, s):
+    def part_ab(q, g, s, i):
         c = 2 * g + s
-        if q == 0:
+        if q == 0 and i == 0:
             pltpu.make_async_copy(gate_up.at[g, s], gate_up.at[g, s], gate_up_sem.at[c]).wait()
-        tok = pair_rows(xc, q)
-        for i in (0, 1):
-            ab_keep[q, c, i], ab_give[q, c, i] = split(_dot(tok, gate_up[g, s, i], 1, 0))
-        core_ab(q, c).start()
+        ab_keep[q, c, i], ab_give[q, c, i] = split(_dot(pair_rows(xc, q), gate_up[g, s, i], 1, 0))
+        core_ab(q, c, i).start()
 
     def part_g(q, g, s):
         c = 2 * g + s
@@ -152,33 +151,32 @@
         each(body)
         second(groups - 1)
 
-    def home_parts(part, send_on):
+    def home_parts(part, send_on, kinds):
+        steps = [(s,) + kind for s in (0, 1) for kind in kinds]
+
         def body(g):
-            part(0, g, 0)
-
-            @pl.when(g > 0)
-            def _():
-                send_on(2 * g - 1)
-            part(0, g, 1)
-            send_on(2 * g)
+            for n, (s, *kind) in enumerate(steps):
+                part(0, g, s, *kind)
+                before_s, *before = steps[n - 1]
+                if n == 0:
+                    pl.when(g > 0)(lambda: send_on(2 * g - 1, *before))
+                else:
+                    send_on(2 * g + before_s, *before)
 
         each(body)
-        send_on(2 * groups - 1)
-
-    def away_parts(part):
-        each(lambda g: (part(1, g, 0), part(1, g, 1)))
+        send_on(2 * groups - 1, *kinds[-1])
 
     token(SIB, 0).wait_recv()
-    home_parts(part_ab, send_ab)
+    home_parts(part_ab, send_ab, ((0,), (1,)))
     for i in (0, 1):
         tokens_far(i).wait_recv()
         token_fwd(i).start()
     token(SIB, 1).wait_recv()
-    home_parts(part_g, send_g)
+    home_parts(part_g, send_g, ((),))
     token_fwd(0).wait_recv()
-    away_parts(part_ab)
+    each(lambda g: [part_ab(1, g, s, i) for s in (0, 1) for i in (0, 1)])
     token_fwd(1).wait_recv()
-    away_parts(part_g)
+    each(lambda g: [part_g(1, g, s) for s in (0, 1)])
     x_t[...] = xc[...].reshape(2 * SHARDS * half, width).T
 
     def hid_far(g):
@@ -227,7 +225,8 @@
     def form_hidden(g):
         for s in (0, 1):
             c = 2 * g + s
-            link_ab(c).wait_recv()
+            for i in (0, 1):
+                link_ab(c, i).wait_recv()
             total = ab_keep[1, c] + ab_got[1, c] + ab_recv[c]
             ab_keep[1, c] = total
             a, b = total[0], total[1]
@@ -432,9 +431,9 @@
             write(n, slot, 2).start()
         return carry
 
-    lax.fori_loop(0, groups, body, 0)
     for copy in rows_out:
         copy.start()
+    lax.fori_loop(0, groups, body, 0)
     for n in range(groups * per_group - RING, groups * per_group):
         for k in range(3):
             write(n, n % RING, k).wait()
@@ -461,7 +460,7 @@
             name='exchange',
             out_shape=(sds((width, tokens), BF16), sds(tok, BF16), sds((groups, 2, SHARDS, half, GROUP), BF16),
                        sds((groups, 2, SHARDS, 2, half, GROUP), BF16), sds(own, BF16), sds(own, BF16)),
-            in_specs=[vmem, hbm, hbm, hbm, vmem],
+            in_specs=[vmem, hbm, hbm, hbm],
             out_specs=[vmem] * 6,
             scratch_shapes=[
                 pltpu.VMEM(tok, BF16),
@@ -476,12 +475,12 @@
                 pltpu.VMEM((SHARDS, half, width), BF16), pltpu.VMEM(block, BF16),
                 pltpu.VMEM((SHARDS, 2, half, width), BF16), pltpu.VMEM((2,) + block, BF16),
                 pltpu.VMEM(block, F32), pltpu.VMEM((2,) + block, F32),
-                dma((SENDS,)), dma((chunks,)), dma((groups,)), dma((2, 3)), dma((2, chunks)), dma((2,)),
-                dma((2, chunks)), dma((3, groups)), dma((2, 2, groups)), dma(()), dma((3,)), dma((3,)), dma((4,)), dma((2, 3)),
+                dma((SENDS,)), dma((chunks,)), dma((groups,)), dma((2, 3)), dma((3, chunks)), dma((2,)),
+                dma((3, chunks)), dma((3, groups)), dma((2, 2, groups)), dma(()), dma((3,)), dma((3,)), dma((4,)), dma((2, 3)),
             ],
             compiler_params=pltpu.CompilerParams(collective_id=0, has_side_effects=True,
                                                  vmem_limit_bytes=44 * 1024 * 1024),
-        )(x_rows.reshape(own), gate_blk, up_blk, down_blk, dy_rows.reshape(own))
+        )(jnp.concatenate([x_rows, dy_rows]).reshape((2,) + own), gate_blk, up_blk, down_blk)
 
         y_new, dx_new, dw_gate, dw_up, dw_down = pl.pallas_call(
             gradient_kernel,

time: 82.9 us -> 81.9 us (0.988)
  local copies, waits for them, and re-layouts: 1.85 us -> 0 us
  other arithmetic: 0 us -> 1.05 us
    unnamed x4 -> x0, local copies, waits for them, and re-layouts: 1.85 us -> none
    concatenate x0 -> x1, other arithmetic: none -> 1.05 us  [device_pass(): jnp.concatenate([x_rows, dy_rows]).reshape((2,) + own)]
where the time goes in v4:
time: 81.9 us; the launch traced here: 81.8 us
  Pallas kernels  80.1 us (98%)
  other arithmetic  1.05 us (1%)
    pallas_call x1, Pallas kernels, device_pass(): pl.pallas_call(exchange_kernel, name='exchange', out_shape=(sds((width, t...  67.5 us
    pallas_call x1, Pallas kernels, device_pass(): pl.pallas_call(gradient_kernel, name='gradients', out_shape=(sds(own, BF1...  12.6 us

profile of v4, /device:TPU:0, one launch (start us, length us, event | category | flops | bytes accessed | tf_op | source)
XLA Modules:
  0.0 81.8 jit_solution(8297619624366897802)
XLA Ops:
  0.6 1.0 %pad_maximum_fusion = bf16[64,3072]{1,0:T(8,128)(2,1)S(1)} fusion(bf16[32,3072]{1,0:T(8,128)(2,1)} %param.9, bf16[32,3072]{1,0:T(8,128)(2,1)} %param.5), kind=kLoop, calls=%fused_computation | loop fusion | flops 786432 | bytes 786432 | tf_op jit(solution)/shard_map/concatenate | solution.py:483
  1.7 67.5 %exchange.1 = (bf16[768,128]{1,0:T(8,128)(2,1)S(1)}, bf16[2,4,16,768]{3,2,1,0:T(8,128)(2,1)S(1)}, bf16[4,2,4,16,1024]{4,3,2,1,0:T(8,128)(2,1)S(1)}, bf16[4,2,4,2...) custom-call(bf16[2,2,16,3072]{3,2,1,0:T(8,128)(2,1)S(1)} %bitcast.3, ...), custom_call_target="tpu_custom_call" | custom-call | tf_op jit(solution)/shard_map/exchange/pallas_call | solution.py:458
  69.2 12.6 %gradients.1 = (bf16[2,16,3072]{2,1,0:T(8,128)(2,1)}, bf16[2,16,3072]{2,1,0:T(8,128)(2,1)}, f32[768,4096]{1,0:T(8,128)}, f32[768,4096]{1,0:T(8,128)}, f32[4096,768]{1,0:T(8,128)}) custom-call(bf16[768,128]{1,0:T(8,128)(2,1)S(1)} %get-tuple-element.16.x_t, bf16[2,4,16,768]{3,2,1,0:T(8,128)(2,1)S(1)} %get-tuple-element.17.dyc, ...), custom_call_target="tpu_custom_call" | custom-call | tf_op jit(solution)/shard_map/gradients/pallas_call | solution.py:485

commit v5 on v4

--- a/solution.py
+++ b/solution.py
@@ -16,7 +16,7 @@
 OWN, SIB, FAR, DIAG = 0, 1, 2, 3
 (S_TOK, S_TOK_FWD, S_CORE_AB, S_CORE_G, S_LINK_AB, S_LINK_G, S_HID_FAR, S_HID_SIB, S_HID_FWD, S_GRAD_FAR, S_GRAD_SIB,
  S_GRAD_FWD, S_TP, S_ROW_HOME, S_ROW_AWAY, S_ROW_FWD, S_TAIL) = (0, 2, 4, 6, 8, 9, 10, 11, 12, 13, 14, 15, 16, 19, 20, 22, 23)
-SENDS = 26
+SENDS = 27
 
 
 def _dot(lhs, rhs, lhs_dim, rhs_dim):
@@ -24,7 +24,7 @@
 
 
 def exchange_kernel(token_rows, gate_hbm, up_hbm, down_hbm,
-                    x_t, dyc, hid, grad, y_rows, dx_rows,
+                    x_t, dyc, hid, grad, y_rows, dx_first, dx_half,
                     xc, gate_up, down,
                     ab_keep, ab_give, ab_got, g_keep, g_give, g_got, ab_recv, g_recv,
                     y_acc, dx_away, dx_home, y_peer, dx_peer, y_sum, dx_sum, y_stage, dx_stage, here_in, near_in,
@@ -93,18 +93,18 @@
             token(p, i).start()
 
     def core_ab(q, c, i):
-        rs = core_rs.at[i, c] if q == 0 else away_rs.at[0]
+        rs = core_rs.at[0, lax.rem(2 * c + i, 4)] if q == 0 else away_rs.at[0]
         return remote(ab_give.at[q, c, i], ab_got.at[q, c, i], S_CORE_AB + q, rs, dp=sib)
 
     def core_g(q, c):
-        rs = core_rs.at[2, c] if q == 0 else away_rs.at[1]
+        rs = core_rs.at[1, lax.rem(c, 4)] if q == 0 else away_rs.at[1]
         return remote(g_give.at[q, c], g_got.at[q, c], S_CORE_G + q, rs, dp=sib)
 
     def link_ab(c, i):
-        return remote(ab_keep.at[0, c, i], ab_recv.at[c, i], S_LINK_AB, link_rs.at[i, c], dp=far)
+        return remote(ab_keep.at[0, c, i], ab_recv.at[c, i], S_LINK_AB, link_rs.at[0, c // 2], dp=far)
 
     def link_g(c):
-        return remote(g_keep.at[0, c], g_recv.at[c], S_LINK_G, link_rs.at[2, c], dp=far)
+        return remote(g_keep.at[0, c], g_recv.at[c], S_LINK_G, link_rs.at[1, c // 2], dp=far)
 
     def send_ab(c, i):
         core_ab(0, c, i).wait_recv()
@@ -223,10 +223,10 @@
         dx_home[h] += part.reshape(dx_home.shape[1:])
 
     def form_hidden(g):
+        both = pl.ds(2 * g, 2)
+        remote(ab_recv.at[both], ab_recv.at[both], S_LINK_AB, link_rs.at[0, g], dp=far).wait_recv()
         for s in (0, 1):
             c = 2 * g + s
-            for i in (0, 1):
-                link_ab(c, i).wait_recv()
             total = ab_keep[1, c] + ab_got[1, c] + ab_recv[c]
             ab_keep[1, c] = total
             a, b = total[0], total[1]
@@ -239,9 +239,10 @@
         add_y(1, g)
 
     def form_grads(g):
+        both = pl.ds(2 * g, 2)
+        remote(g_recv.at[both], g_recv.at[both], S_LINK_G, link_rs.at[1, g], dp=far).wait_recv()
         for s in (0, 1):
             c = 2 * g + s
-            link_g(c).wait_recv()
             v = g_keep[1, c] + g_got[1, c] + g_recv[c]
             a, b = ab_keep[1, c, 0], ab_keep[1, c, 1]
             sig = jax.nn.sigmoid(a)
@@ -273,14 +274,11 @@
     def y_away_fwd():
         return remote(y_stage.at[2:4, 0], y_stage.at[2:4, 1], S_ROW_FWD, away_row_rs.at[1], tp=1 - tp)
 
-    def dx_row(p, r):
-        device = {'dp': peers[p]}
-        if r:
-            device['tp'] = 1 - tp
-        return remote(dx_sum.at[p - 2], dx_stage.at[r, p - 2], S_ROW_AWAY + 1, away_row_rs.at[2 + r], **device)
-
-    def dx_row_all(r):
-        return remote(dx_sum, dx_stage.at[r], S_ROW_AWAY + 1, away_row_rs.at[2 + r], dp=far)
+    def dx_row(p):
+        return remote(dx_sum.at[p - 2], dx_stage.at[p - 2], S_ROW_AWAY + 1, away_row_rs.at[2], dp=peers[p])
+
+    def dx_row_all():
+        return remote(dx_sum, dx_stage, S_ROW_AWAY + 1, away_row_rs.at[2], dp=far)
 
     def finish_y(q):
         y_tp[q].wait()
@@ -293,16 +291,19 @@
             for p in (FAR, DIAG):
                 y_away(p).start()
 
-    def tail(h):
-        return (remote(dx_home.at[h, 0], here_in.at[h], S_TAIL, tail_rs.at[h, 0], tp=1 - tp),
-                remote(dx_home.at[h, 1], near_in.at[h, 1], S_TAIL + 1, tail_rs.at[h, 1], dp=sib, tp=1 - tp),
-                remote(dx_home.at[h, 1], near_in.at[h, 0], S_TAIL + 2, tail_rs.at[h, 2], dp=sib))
-
-    def finish_dx_home(h):
-        for copy in tail(h):
-            copy.wait_recv()
-        dx_rows[h, :, cols(dp)] = (dyc[h, OWN].astype(F32) + (dx_home[h, 0] + here_in[h])).astype(BF16)
-        dx_rows[h, :, cols(sib)] = (dy_own[h, :, cols(sib)].astype(F32) + (near_in[h, 0] + near_in[h, 1])).astype(BF16)
+    def tail():
+        return (remote(dx_home.at[0, 0], here_in, S_TAIL, tail_rs.at[0], tp=1 - tp),
+                remote(dx_home.at[0, 1], near_in.at[1], S_TAIL + 1, tail_rs.at[1], dp=sib, tp=1 - tp),
+                remote(dx_home.at[0, 1], near_in.at[0], S_TAIL + 2, tail_rs.at[2], dp=sib))
+
+    def swap():
+        return remote(dx_home.at[1, 1], dx_half.at[SIB], S_TAIL + 3, tail_rs.at[3], dp=sib)
+
+    def finish_dx_first():
+        for copy in tail():
+            copy.wait()
+        dx_first[0] = (dyc[0, OWN].astype(F32) + (dx_home[0, 0] + here_in[...])).astype(BF16)
+        dx_first[1] = (dy_own[0, :, cols(sib)].astype(F32) + (near_in[0] + near_in[1])).astype(BF16)
 
     remote(ab_give.at[1], ab_got.at[1], S_CORE_AB + 1, away_rs.at[0], dp=sib).wait()
     behind(form_hidden, away_y)
@@ -339,7 +340,7 @@
         return body
 
     behind(take_grad(0), home_dx(0))
-    for copy in tail(0):
+    for copy in tail():
         copy.start()
     finish_y(0)
     y_away_all().wait_recv()
@@ -355,14 +356,12 @@
         @pl.when(g == groups - 1)
         def _():
             for p in (FAR, DIAG):
-                for r in (1, 0):
-                    dx_row(p, r).start()
+                dx_row(p).start()
 
     behind(last_grads, each_home)
-    for copy in tail(1):
-        copy.start()
-
-    finish_dx_home(0)
+    swap().start()
+    dx_half[OWN] = dx_home[1, 0]
+    finish_dx_first()
     for p, r in home_rows:
         row_home(p, r).wait_recv()
     y_away_fwd().wait_recv()
@@ -386,25 +385,19 @@
     remote(y_sum.at[0:3], y_sum.at[0:3], S_ROW_HOME, home_rs.at[0], dp=sib).wait_send()
     y_away_all().wait_send()
     y_away_fwd().wait_send()
-    remote(dx_stage, dx_stage, S_ROW_AWAY + 1, away_row_rs.at[2], dp=far).wait_send()
-
-    for r in (0, 1):
-        dx_row_all(r).wait_recv()
-    for p in (FAR, DIAG):
-        dx_rows[tp, :, cols(owner[p])] = dx_stage[0, p - 2]
-        dx_rows[1 - tp, :, cols(owner[p])] = dx_stage[1, p - 2]
-    finish_dx_home(1)
-    for k in range(3):
-        remote(dx_home.at[:, 0], here_in, S_TAIL + k, tail_rs.at[0, 0], dp=sib).wait_send()
-
-
-def gradient_kernel(x_t, dyc, hid, grad, y_rows, dx_rows, y_out, dx_out, dgate_out, dup_out, ddown_out,
+
+    dx_row_all().wait()
+    dx_half[2:4] = dx_stage[...].astype(F32)
+    swap().wait()
+
+
+def gradient_kernel(x_t, dyc, hid, grad, y_rows, y_out, dgate_out, dup_out, ddown_out,
                     dgate, dup, ddown, row_sem, tile_sem):
     groups = hid.shape[0]
     tokens = x_t.shape[1]
     width = dyc.shape[-1]
     per_group = GROUP // TILE
-    rows_out = [pltpu.make_async_copy(y_rows, y_out, row_sem.at[0]), pltpu.make_async_copy(dx_rows, dx_out, row_sem.at[1])]
+    rows_out = pltpu.make_async_copy(y_rows, y_out, row_sem)
 
     def write(n, slot, k):
         at = pl.ds(pl.multiple_of(n * TILE, TILE), TILE)
@@ -431,14 +424,29 @@
             write(n, slot, 2).start()
         return carry
 
-    for copy in rows_out:
-        copy.start()
+    rows_out.start()
     lax.fori_loop(0, groups, body, 0)
     for n in range(groups * per_group - RING, groups * per_group):
         for k in range(3):
             write(n, n % RING, k).wait()
-    for copy in rows_out:
-        copy.wait()
+    rows_out.wait()
+
+
+def place_kernel(token_rows, dx_first, mine, theirs, dx_out):
+    tp = lax.axis_index('tp')
+    dp = lax.axis_index('dp')
+    sib = dp + 1 - 2 * lax.rem(dp, 2)
+    width = mine.shape[-1]
+
+    def cols(i):
+        return pl.ds(pl.multiple_of(i * width, width), width)
+
+    for p, owner in ((OWN, dp), (SIB, sib)):
+        dx_out[0, :, cols(owner)] = dx_first[p]
+        dx_out[1, :, cols(owner)] = (token_rows[1, 1, :, cols(owner)].astype(F32) + (mine[p] + theirs[p])).astype(BF16)
+    for p, owner in ((FAR, lax.rem(dp + 2, SHARDS)), (DIAG, lax.rem(sib + 2, SHARDS))):
+        dx_out[tp, :, cols(owner)] = mine[p].astype(BF16)
+        dx_out[1 - tp, :, cols(owner)] = theirs[p].astype(BF16)
 
 
 def solution(mesh):
@@ -455,13 +463,15 @@
         tok = (2, SHARDS, half, width)
         block = (2, half, width)
         own = (2, half, model)
-        x_t, dyc, hid, grad, y_own, dx_own = pl.pallas_call(
+        token_rows = jnp.concatenate([x_rows, dy_rows]).reshape((2,) + own)
+        x_t, dyc, hid, grad, y_own, dx_first, dx_half = pl.pallas_call(
             exchange_kernel,
             name='exchange',
             out_shape=(sds((width, tokens), BF16), sds(tok, BF16), sds((groups, 2, SHARDS, half, GROUP), BF16),
-                       sds((groups, 2, SHARDS, 2, half, GROUP), BF16), sds(own, BF16), sds(own, BF16)),
+                       sds((groups, 2, SHARDS, 2, half, GROUP), BF16), sds(own, BF16), sds(block, BF16),
+                       sds((SHARDS, half, width), F32)),
             in_specs=[vmem, hbm, hbm, hbm],
-            out_specs=[vmem] * 6,
+            out_specs=[vmem] * 7,
             scratch_shapes=[
                 pltpu.VMEM(tok, BF16),
                 pltpu.VMEM((groups, 2, 2, width, CHUNK), BF16), pltpu.VMEM((groups, GROUP, width), BF16),
@@ -473,26 +483,36 @@
                 pltpu.VMEM((2, 2) + block, F32), pltpu.VMEM((2,) + block, F32), pltpu.VMEM((2,) + block, F32),
                 pltpu.VMEM((2,) + block, F32), pltpu.VMEM(block, F32),
                 pltpu.VMEM((SHARDS, half, width), BF16), pltpu.VMEM(block, BF16),
-                pltpu.VMEM((SHARDS, 2, half, width), BF16), pltpu.VMEM((2,) + block, BF16),
-                pltpu.VMEM(block, F32), pltpu.VMEM((2,) + block, F32),
-                dma((SENDS,)), dma((chunks,)), dma((groups,)), dma((2, 3)), dma((3, chunks)), dma((2,)),
-                dma((3, chunks)), dma((3, groups)), dma((2, 2, groups)), dma(()), dma((3,)), dma((3,)), dma((4,)), dma((2, 3)),
+                pltpu.VMEM((SHARDS, 2, half, width), BF16), pltpu.VMEM(block, BF16),
+                pltpu.VMEM((half, width), F32), pltpu.VMEM(block, F32),
+                dma((SENDS,)), dma((chunks,)), dma((groups,)), dma((2, 3)), dma((2, 4)), dma((2,)),
+                dma((2, groups)), dma((3, groups)), dma((2, 2, groups)), dma(()), dma((3,)), dma((3,)), dma((3,)), dma((4,)),
             ],
             compiler_params=pltpu.CompilerParams(collective_id=0, has_side_effects=True,
                                                  vmem_limit_bytes=44 * 1024 * 1024),
-        )(jnp.concatenate([x_rows, dy_rows]).reshape((2,) + own), gate_blk, up_blk, down_blk)
-
-        y_new, dx_new, dw_gate, dw_up, dw_down = pl.pallas_call(
+        )(token_rows, gate_blk, up_blk, down_blk)
+        dx_other = lax.ppermute(dx_half, 'tp', [(0, 1), (1, 0)])
+
+        y_new, dw_gate, dw_up, dw_down = pl.pallas_call(
             gradient_kernel,
             name='gradients',
-            out_shape=(sds(own, BF16), sds(own, BF16), sds((width, hidden), F32), sds((width, hidden), F32),
-                       sds((hidden, width), F32)),
-            in_specs=[vmem] * 6,
-            out_specs=[hbm] * 5,
+            out_shape=(sds(own, BF16), sds((width, hidden), F32), sds((width, hidden), F32), sds((hidden, width), F32)),
+            in_specs=[vmem] * 5,
+            out_specs=[hbm] * 4,
             scratch_shapes=[pltpu.VMEM((RING, width, TILE), F32), pltpu.VMEM((RING, width, TILE), F32),
-                            pltpu.VMEM((RING, TILE, width), F32), dma((2,)), dma((3, RING))],
+                            pltpu.VMEM((RING, TILE, width), F32), dma(()), dma((3, RING))],
+            cost_estimate=pl.CostEstimate(flops=6 * tokens * width * hidden, bytes_accessed=12 * width * hidden,
+                                          transcendentals=0),
             compiler_params=pltpu.CompilerParams(vmem_limit_bytes=44 * 1024 * 1024),
-        )(x_t, dyc, hid, grad, y_own, dx_own)
+        )(x_t, dyc, hid, grad, y_own)
+        dx_new = pl.pallas_call(
+            place_kernel,
+            name='place_dx',
+            out_shape=sds(own, BF16),
+            in_specs=[vmem] * 4,
+            out_specs=vmem,
+            compiler_params=pltpu.CompilerParams(vmem_limit_bytes=4 * 1024 * 1024),
+        )(token_rows, dx_first, dx_half, dx_other)
         return y_new.reshape(rows, model), dx_new.reshape(rows, model), dw_gate, dw_up, dw_down
 
     row_spec = P('dp', None)

time: 81.9 us -> 80.3 us (0.980)
  Pallas kernels: 80.1 us -> 77.4 us
  starting transfers between devices: 0 us -> 1.04 us
    pallas_call x1, Pallas kernels: 67.5 us -> 64.1 us  [device_pass(): pl.pallas_call(exchange_kernel, name='exchange', out_shape=(sds((width, t...]
    ppermute x0 -> x1, starting transfers between devices: none -> 1.04 us  [device_pass(): dx_other = lax.ppermute(dx_half, 'tp', [(0, 1), (1, 0)])]
  transfers between devices with their start and end apart: 0 -> 1, of which waited for: 0 -> 0; matrix products, arithmetic and copies ran while one was open for 0% -> 0% of each run, Pallas kernels for 0% -> 16%
where the time goes in v5:
time: 80.3 us; the launch traced here: 80.2 us
  Pallas kernels  77.4 us (96%)
  other arithmetic  1.05 us (1%)
  starting transfers between devices  1.04 us (1%)
    pallas_call x1, Pallas kernels, device_pass(): pl.pallas_call(exchange_kernel, name='exchange', out_shape=(sds((width, t...  64.1 us
    pallas_call x1, Pallas kernels, device_pass(): pl.pallas_call(gradient_kernel, name='gradients', out_shape=(sds(own, BF1...  12.6 us
  transfers between devices with their start and end apart: 1, of which 0 were waited for; matrix products, arithmetic and copies ran while one was open for 0% of the time, Pallas kernels for 16%

profile of v5, /device:TPU:0, one launch (start us, length us, event | category | flops | bytes accessed | tf_op | source)
XLA Modules:
  0.0 80.2 jit_solution(12557938190732985480)
XLA Ops:
  0.6 1.0 %pad_maximum_fusion = bf16[64,3072]{1,0:T(8,128)(2,1)S(1)} fusion(bf16[32,3072]{1,0:T(8,128)(2,1)} %param.9, bf16[32,3072]{1,0:T(8,128)(2,1)} %param.5), kind=kLoop, calls=%fused_computation | loop fusion | flops 786432 | bytes 786432 | tf_op jit(solution)/shard_map/concatenate | solution.py:466
  1.7 64.1 %exchange.1 = (bf16[768,128]{1,0:T(8,128)(2,1)S(1)}, bf16[2,4,16,768]{3,2,1,0:T(8,128)(2,1)S(1)}, bf16[4,2,4,16,1024]{4,3,2,1,0:T(8,128)(2,1)S(1)}, bf16[4,2,4,2...) custom-call(bf16[2,2,16,3072]{3,2,1,0:T(8,128)(2,1)S(1)} %bitcast.3,, ...), custom_call_target="tpu_custom_call" | custom-call | tf_op jit(solution)/shard_map/exchange/pallas_call | solution.py:467
  65.8 1.0 %collective-permute-start = (f32[4,16,768]{2,1,0:T(8,128)S(1)}, f32[4,16,768]{2,1,0:T(8,128)S(1)}, u32[]{:S(2)}, u32[]{:S(2)}) collective-permute-start(f32[4,16,768]{2,1,0:T(8,128)S(1)} %get-tuple-element.23.mine), channel_id=1, source_target_pairs={{0,4},{4,0},{1,5},{5,1},{2,6},{6,2},{3,7},{7,3}} | collective-permute-start | bytes 589832 | tf_op jit(solution)/shard_map/ppermute | solution.py:494
  66.9 12.6 %gradients.1 = (bf16[2,16,3072]{2,1,0:T(8,128)(2,1)}, f32[768,4096]{1,0:T(8,128)}, f32[768,4096]{1,0:T(8,128)}, f32[4096,768]{1,0:T(8,128)}) custom-call(bf16[768,128]{1,0:T(8,128)(2,1)S(1)} %get-tuple-element.16.x_t, bf16[2,4,16,768]{3,2,1,0:T(8,128)(2,1)S(1)} %get-tuple-element.17.dyc, bf16[4,2,4,16,1024]{4,3,2,1,0:T(8,128)(2,1)S(1)} %get-tuple-element.18.hid, ...), custom_call_target="tpu_custom_call" | custom-call | flops 2415919104 | bytes 37748736 | tf_op jit(solution)/shard_map/gradients/pallas_call | solution.py:496
  79.4 0.0 collective-permute-done.theirs
  79.5 0.7 place_dx.1
Async XLA Ops:
  65.8 13.6 %collective-permute-start = (f32[4,16,768]{2,1,0:T(8,128)S(1)}, f32[4,16,768]{2,1,0:T(8,128)S(1)}, u32[]{:S(2)}, u32[]{:S(2)}) collective-permute-start(f32[4,16,768]{2,1,0:T(8,128)S(1)} %get-tuple-element.23.mine), channel_id=1, source_target_pairs={{0,4},{4,0},{1,5},{5,1},{2,6},{6,2},{3,7},{7,3}} | collective-permute-start | bytes 589832 | tf_op jit(solution)/shard_map/ppermute | solution.py:494

commit v6 on v5

--- a/solution.py
+++ b/solution.py
@@ -11,12 +11,12 @@
 SHARDS = 4
 CHUNK = 512
 GROUP = 2 * CHUNK
-TILE = 512
+TILE = CHUNK
 RING = 3
 OWN, SIB, FAR, DIAG = 0, 1, 2, 3
 (S_TOK, S_TOK_FWD, S_CORE_AB, S_CORE_G, S_LINK_AB, S_LINK_G, S_HID_FAR, S_HID_SIB, S_HID_FWD, S_GRAD_FAR, S_GRAD_SIB,
- S_GRAD_FWD, S_TP, S_ROW_HOME, S_ROW_AWAY, S_ROW_FWD, S_TAIL) = (0, 2, 4, 6, 8, 9, 10, 11, 12, 13, 14, 15, 16, 19, 20, 22, 23)
-SENDS = 27
+ S_GRAD_FWD, S_TP, S_ROW_HOME, S_ROW_AWAY, S_SWAP) = (0, 2, 4, 6, 8, 9, 10, 11, 12, 13, 14, 15, 16, 19, 20, 22)
+SENDS = 23
 
 
 def _dot(lhs, rhs, lhs_dim, rhs_dim):
@@ -24,12 +24,12 @@
 
 
 def exchange_kernel(token_rows, gate_hbm, up_hbm, down_hbm,
-                    x_t, dyc, hid, grad, y_rows, dx_first, dx_half,
+                    x_t, dyc, hid, grad, y_home, half_rows,
                     xc, gate_up, down,
                     ab_keep, ab_give, ab_got, g_keep, g_give, g_got, ab_recv, g_recv,
-                    y_acc, dx_away, dx_home, y_peer, dx_peer, y_sum, dx_sum, y_stage, dx_stage, here_in, near_in,
+                    y_acc, dx_away, dx_home, y_peer, dx_peer, y_sum, dx_sum, y_far, dx_far,
                     send, gate_up_sem, down_sem, tok_rs, core_rs, away_rs, link_rs,
-                    hid_rs, grad_rs, grad_sib_rs, tp_rs, home_rs, away_row_rs, tail_rs):
+                    hid_rs, grad_rs, grad_sib_rs, tp_rs, home_rs, away_row_rs, swap_rs):
     tp = lax.axis_index('tp')
     dp = lax.axis_index('dp')
     sib = dp + 1 - 2 * lax.rem(dp, 2)
@@ -188,14 +188,14 @@
     def hid_fwd(g):
         return remote(hid.at[g, :, OWN], hid.at[g, :, SIB], S_HID_FWD, hid_rs.at[2, g], dp=sib)
 
-    def grad_far(g, h):
-        return remote(grad.at[g, h, FAR], grad.at[g, h, OWN], S_GRAD_FAR, grad_rs.at[0, h, g], dp=far)
-
-    def grad_sib(g):
-        return remote(grad.at[g, :, FAR], grad.at[g, :, DIAG], S_GRAD_SIB, grad_sib_rs, dp=sib)
-
-    def grad_fwd(g, h):
-        return remote(grad.at[g, h, OWN], grad.at[g, h, SIB], S_GRAD_FWD, grad_rs.at[1, h, g], dp=sib)
+    def grad_far(c):
+        return remote(grad.at[c, :, FAR], grad.at[c, :, OWN], S_GRAD_FAR, grad_rs.at[0, c], dp=far)
+
+    def grad_sib(c):
+        return remote(grad.at[c, :, FAR], grad.at[c, :, DIAG], S_GRAD_SIB, grad_sib_rs, dp=sib)
+
+    def grad_fwd(c):
+        return remote(grad.at[c, :, OWN], grad.at[c, :, SIB], S_GRAD_FWD, grad_rs.at[1, c], dp=sib)
 
     y_acc[...] = jnp.zeros_like(y_acc)
     dx_away[...] = jnp.zeros_like(dx_away)
@@ -205,22 +205,13 @@
         part = _dot(hid[g, :, 2 * q:2 * q + 2].reshape(4 * half, GROUP), down[g], 1, 0)
         y_acc[q] += part.reshape(y_acc.shape[1:])
 
-    def dx_part(take, count, g):
+    def add_dx(acc, q, g, s):
         part = None
-        for s in (0, 1):
-            for i in (0, 1):
-                lhs = take(i, s * CHUNK).reshape(count, CHUNK)
-                term = _dot(lhs, gate_up[g, s, i], 1, 1)
-                part = term if part is None else part + term
-        return part
-
-    def add_dx_away(g):
-        part = dx_part(lambda i, at: grad[g, :, 2:4, i, :, at:at + CHUNK], 4 * half, g)
-        dx_away[...] += part.reshape(dx_away.shape)
-
-    def add_dx_home(g, h):
-        part = dx_part(lambda i, at: grad[g, h, 0:2, i, :, at:at + CHUNK], 2 * half, g)
-        dx_home[h] += part.reshape(dx_home.shape[1:])
+        for i in (0, 1):
+            lhs = grad[2 * g + s, :, 2 * q:2 * q + 2, i].reshape(4 * half, CHUNK)
+            term = _dot(lhs, gate_up[g, s, i], 1, 1)
+            part = term if part is None else part + term
+        acc[...] += part.reshape(acc.shape)
 
     def form_hidden(g):
         both = pl.ds(2 * g, 2)
@@ -246,10 +237,10 @@
             v = g_keep[1, c] + g_got[1, c] + g_recv[c]
             a, b = ab_keep[1, c, 0], ab_keep[1, c, 1]
             sig = jax.nn.sigmoid(a)
-            grad[g, :, FAR, 0, :, s * CHUNK:(s + 1) * CHUNK] = (v * b * sig * (1.0 + a * (1.0 - sig))).astype(BF16)
-            grad[g, :, FAR, 1, :, s * CHUNK:(s + 1) * CHUNK] = (v * (a * sig)).astype(BF16)
-        grad_far(g, 0).start()
-        grad_sib(g).start()
+            grad[c, :, FAR, 0] = (v * b * sig * (1.0 + a * (1.0 - sig))).astype(BF16)
+            grad[c, :, FAR, 1] = (v * (a * sig)).astype(BF16)
+            grad_far(c).start()
+            grad_sib(c).start()
 
     def tp_copy(acc, peer, k):
         return remote(acc.at[1 - tp], peer, S_TP + k, tp_rs.at[k], tp=1 - tp)
@@ -261,49 +252,28 @@
         device = {} if p == OWN else {'dp': sib}
         if r:
             device['tp'] = 1 - tp
-        return remote(y_sum.at[p], y_stage.at[p, r], S_ROW_HOME, home_rs.at[2 if p == OWN else r], **device)
+        return remote(y_sum.at[p], y_home.at[p, r], S_ROW_HOME, home_rs.at[2 if p == OWN else r], **device)
 
     home_rows = ((OWN, 1), (SIB, 0), (SIB, 1))
 
-    def y_away(p):
-        return remote(y_sum.at[p], y_stage.at[p, 0], S_ROW_AWAY, away_row_rs.at[0], dp=peers[p])
-
-    def y_away_all():
-        return remote(y_sum.at[2:4], y_stage.at[2:4, 0], S_ROW_AWAY, away_row_rs.at[0], dp=far)
-
-    def y_away_fwd():
-        return remote(y_stage.at[2:4, 0], y_stage.at[2:4, 1], S_ROW_FWD, away_row_rs.at[1], tp=1 - tp)
-
-    def dx_row(p):
-        return remote(dx_sum.at[p - 2], dx_stage.at[p - 2], S_ROW_AWAY + 1, away_row_rs.at[2], dp=peers[p])
-
-    def dx_row_all():
-        return remote(dx_sum, dx_stage, S_ROW_AWAY + 1, away_row_rs.at[2], dp=far)
+    def far_row(i, p):
+        total = y_sum.at[p] if i == 0 else dx_sum.at[p - 2]
+        return remote(total, (y_far, dx_far)[i].at[p - 2], S_ROW_AWAY + i, away_row_rs.at[i], dp=peers[p])
+
+    def far_rows(i):
+        rows_in = (y_far, dx_far)[i]
+        return remote(rows_in, rows_in, S_ROW_AWAY + i, away_row_rs.at[i], dp=far)
 
     def finish_y(q):
         y_tp[q].wait()
         y_sum[2 * q:2 * q + 2] = (xc[tp, 2 * q:2 * q + 2].astype(F32) + (y_acc[q, tp] + y_peer[q])).astype(BF16)
         if q == 0:
-            y_stage[OWN, 0] = y_sum[OWN]
+            y_home[OWN, 0] = y_sum[OWN]
             for p, r in home_rows:
                 row_home(p, r).start()
-        else:
-            for p in (FAR, DIAG):
-                y_away(p).start()
-
-    def tail():
-        return (remote(dx_home.at[0, 0], here_in, S_TAIL, tail_rs.at[0], tp=1 - tp),
-                remote(dx_home.at[0, 1], near_in.at[1], S_TAIL + 1, tail_rs.at[1], dp=sib, tp=1 - tp),
-                remote(dx_home.at[0, 1], near_in.at[0], S_TAIL + 2, tail_rs.at[2], dp=sib))
 
     def swap():
-        return remote(dx_home.at[1, 1], dx_half.at[SIB], S_TAIL + 3, tail_rs.at[3], dp=sib)
-
-    def finish_dx_first():
-        for copy in tail():
-            copy.wait()
-        dx_first[0] = (dyc[0, OWN].astype(F32) + (dx_home[0, 0] + here_in[...])).astype(BF16)
-        dx_first[1] = (dy_own[0, :, cols(sib)].astype(F32) + (near_in[0] + near_in[1])).astype(BF16)
+        return remote(dx_home.at[:, 1], half_rows.at[2:4], S_SWAP, swap_rs, dp=sib)
 
     remote(ab_give.at[1], ab_got.at[1], S_CORE_AB + 1, away_rs.at[0], dp=sib).wait()
     behind(form_hidden, away_y)
@@ -311,7 +281,6 @@
     remote(g_give.at[1], g_got.at[1], S_CORE_G + 1, away_rs.at[1], dp=sib).wait()
     each(form_grads)
     finish_y(1)
-    each(lambda g: grad_far(g, 1).start())
 
     def take_hidden(g):
         hid_far(g).wait_recv()
@@ -320,55 +289,47 @@
     def home_y(g):
         hid_fwd(g).wait_recv()
         add_y(0, g)
-        add_dx_away(g)
+        for s in (0, 1):
+            add_dx(dx_away, 1, g, s)
 
     remote(grad.at[:, :, FAR], grad.at[:, :, DIAG], S_GRAD_SIB, grad_sib_rs, dp=sib).wait()
     behind(take_hidden, home_y)
     y_tp[0].start()
     dx_tp.start()
 
-    def take_grad(h):
-        def body(g):
-            grad_far(g, h).wait_recv()
-            grad_fwd(g, h).start()
-        return body
-
-    def home_dx(h):
-        def body(g):
-            grad_fwd(g, h).wait_recv()
-            add_dx_home(g, h)
-        return body
-
-    behind(take_grad(0), home_dx(0))
-    for copy in tail():
-        copy.start()
-    finish_y(0)
-    y_away_all().wait_recv()
-    y_away_fwd().start()
-    dx_tp.wait()
-    dx_sum[...] = (dyc[tp, 2:4].astype(F32) + (dx_away[tp] + dx_peer[...])).astype(BF16)
-
-    each_home = home_dx(1)
-
-    def last_grads(g):
-        take_grad(1)(g)
-
-        @pl.when(g == groups - 1)
+    def take_grad(c):
+        grad_far(c).wait_recv()
+        grad_fwd(c).start()
+
+    def home_dx(g, s):
+        grad_fwd(2 * g + s).wait_recv()
+        add_dx(dx_home, 0, g, s)
+
+    def take_grads(g):
+        take_grad(2 * g)
+
+        @pl.when(g > 0)
         def _():
-            for p in (FAR, DIAG):
-                dx_row(p).start()
-
-    behind(last_grads, each_home)
+            home_dx(g - 1, 1)
+
+        @pl.when(g == 2)
+        def _():
+            dx_tp.wait()
+            dx_sum[...] = (dyc[tp, 2:4].astype(F32) + (dx_away[tp] + dx_peer[...])).astype(BF16)
+            for i in (0, 1):
+                for p in (FAR, DIAG):
+                    far_row(i, p).start()
+            finish_y(0)
+
+        take_grad(2 * g + 1)
+        home_dx(g, 0)
+
+    each(take_grads)
+    home_dx(groups - 1, 1)
     swap().start()
-    dx_half[OWN] = dx_home[1, 0]
-    finish_dx_first()
+    half_rows[0:2] = dx_home[:, 0]
     for p, r in home_rows:
         row_home(p, r).wait_recv()
-    y_away_fwd().wait_recv()
-    owner = {OWN: dp, SIB: sib, FAR: far, DIAG: diag}
-    for p in range(SHARDS):
-        y_rows[tp, :, cols(owner[p])] = y_stage[p, 0]
-        y_rows[1 - tp, :, cols(owner[p])] = y_stage[p, 1]
 
     for i in (0, 1):
         slots = tokens[i][1]
@@ -383,21 +344,18 @@
     for kind in (S_GRAD_FAR, S_GRAD_FWD):
         remote(grad.at[:, :, OWN], grad.at[:, :, SIB], kind, grad_sib_rs, dp=sib).wait_send()
     remote(y_sum.at[0:3], y_sum.at[0:3], S_ROW_HOME, home_rs.at[0], dp=sib).wait_send()
-    y_away_all().wait_send()
-    y_away_fwd().wait_send()
-
-    dx_row_all().wait()
-    dx_half[2:4] = dx_stage[...].astype(F32)
+
+    for i, rows_in in enumerate((y_far, dx_far)):
+        far_rows(i).wait()
+        half_rows[4 + 2 * i:6 + 2 * i] = rows_in[...].astype(F32)
     swap().wait()
 
 
-def gradient_kernel(x_t, dyc, hid, grad, y_rows, y_out, dgate_out, dup_out, ddown_out,
-                    dgate, dup, ddown, row_sem, tile_sem):
+def gradient_kernel(x_t, dyc, hid, grad, dgate_out, dup_out, ddown_out, dgate, dup, ddown, tile_sem):
     groups = hid.shape[0]
     tokens = x_t.shape[1]
     width = dyc.shape[-1]
     per_group = GROUP // TILE
-    rows_out = pltpu.make_async_copy(y_rows, y_out, row_sem)
 
     def write(n, slot, k):
         at = pl.ds(pl.multiple_of(n * TILE, TILE), TILE)
@@ -417,22 +375,20 @@
             at = slice(s * TILE, (s + 1) * TILE)
             for k, buf in enumerate((dgate, dup)):
                 take(k)
-                buf[slot] = _dot(x_t[...], grad[g, :, :, k, :, at].reshape(tokens, TILE), 1, 0)
+                buf[slot] = _dot(x_t[...], grad[n, :, :, k].reshape(tokens, TILE), 1, 0)
                 write(n, slot, k).start()
             take(2)
             ddown[slot] = _dot(hid[g, :, :, :, at].reshape(tokens, TILE), dyc[...].reshape(tokens, width), 0, 0)
             write(n, slot, 2).start()
         return carry
 
-    rows_out.start()
     lax.fori_loop(0, groups, body, 0)
     for n in range(groups * per_group - RING, groups * per_group):
         for k in range(3):
             write(n, n % RING, k).wait()
-    rows_out.wait()
-
-
-def place_kernel(token_rows, dx_first, mine, theirs, dx_out):
+
+
+def place_kernel(token_rows, y_home, mine, theirs, y_out, dx_out):
     tp = lax.axis_index('tp')
     dp = lax.axis_index('dp')
     sib = dp + 1 - 2 * lax.rem(dp, 2)
@@ -442,11 +398,14 @@
         return pl.ds(pl.multiple_of(i * width, width), width)
 
     for p, owner in ((OWN, dp), (SIB, sib)):
-        dx_out[0, :, cols(owner)] = dx_first[p]
-        dx_out[1, :, cols(owner)] = (token_rows[1, 1, :, cols(owner)].astype(F32) + (mine[p] + theirs[p])).astype(BF16)
+        y_out[tp, :, cols(owner)] = y_home[p, 0]
+        y_out[1 - tp, :, cols(owner)] = y_home[p, 1]
+        at = pl.ds(2 * p, 2)
+        dx_out[:, :, cols(owner)] = (token_rows[1, :, :, cols(owner)].astype(F32) + (mine[at] + theirs[at])).astype(BF16)
     for p, owner in ((FAR, lax.rem(dp + 2, SHARDS)), (DIAG, lax.rem(sib + 2, SHARDS))):
-        dx_out[tp, :, cols(owner)] = mine[p].astype(BF16)
-        dx_out[1 - tp, :, cols(owner)] = theirs[p].astype(BF16)
+        for out, at in ((y_out, p + 2), (dx_out, p + 4)):
+            out[tp, :, cols(owner)] = mine[at].astype(BF16)
+            out[1 - tp, :, cols(owner)] = theirs[at].astype(BF16)
 
 
 def solution(mesh):
@@ -464,14 +423,14 @@
         block = (2, half, width)
         own = (2, half, model)
         token_rows = jnp.concatenate([x_rows, dy_rows]).reshape((2,) + own)
-        x_t, dyc, hid, grad, y_own, dx_first, dx_half = pl.pallas_call(
+        x_t, dyc, hid, grad, y_home, half_rows = pl.pallas_call(
             exchange_kernel,
             name='exchange',
             out_shape=(sds((width, tokens), BF16), sds(tok, BF16), sds((groups, 2, SHARDS, half, GROUP), BF16),
-                       sds((groups, 2, SHARDS, 2, half, GROUP), BF16), sds(own, BF16), sds(block, BF16),
-                       sds((SHARDS, half, width), F32)),
+                       sds((chunks, 2, SHARDS, 2, half, CHUNK), BF16), sds((2,) + block, BF16),
+                       sds((8, half, width), F32)),
             in_specs=[vmem, hbm, hbm, hbm],
-            out_specs=[vmem] * 7,
+            out_specs=[vmem] * 6,
             scratch_shapes=[
                 pltpu.VMEM(tok, BF16),
                 pltpu.VMEM((groups, 2, 2, width, CHUNK), BF16), pltpu.VMEM((groups, GROUP, width), BF16),
@@ -483,36 +442,35 @@
                 pltpu.VMEM((2, 2) + block, F32), pltpu.VMEM((2,) + block, F32), pltpu.VMEM((2,) + block, F32),
                 pltpu.VMEM((2,) + block, F32), pltpu.VMEM(block, F32),
                 pltpu.VMEM((SHARDS, half, width), BF16), pltpu.VMEM(block, BF16),
-                pltpu.VMEM((SHARDS, 2, half, width), BF16), pltpu.VMEM(block, BF16),
-                pltpu.VMEM((half, width), F32), pltpu.VMEM(block, F32),
+                pltpu.VMEM(block, BF16), pltpu.VMEM(block, BF16),
                 dma((SENDS,)), dma((chunks,)), dma((groups,)), dma((2, 3)), dma((2, 4)), dma((2,)),
-                dma((2, groups)), dma((3, groups)), dma((2, 2, groups)), dma(()), dma((3,)), dma((3,)), dma((3,)), dma((4,)),
+                dma((2, groups)), dma((3, groups)), dma((2, chunks)), dma(()), dma((3,)), dma((3,)), dma((2,)), dma(()),
             ],
             compiler_params=pltpu.CompilerParams(collective_id=0, has_side_effects=True,
                                                  vmem_limit_bytes=44 * 1024 * 1024),
         )(token_rows, gate_blk, up_blk, down_blk)
-        dx_other = lax.ppermute(dx_half, 'tp', [(0, 1), (1, 0)])
-
-        y_new, dw_gate, dw_up, dw_down = pl.pallas_call(
+        other_rows = lax.ppermute(half_rows, 'tp', [(0, 1), (1, 0)])
+
+        dw_gate, dw_up, dw_down = pl.pallas_call(
             gradient_kernel,
             name='gradients',
-            out_shape=(sds(own, BF16), sds((width, hidden), F32), sds((width, hidden), F32), sds((hidden, width), F32)),
-            in_specs=[vmem] * 5,
-            out_specs=[hbm] * 4,
+            out_shape=(sds((width, hidden), F32), sds((width, hidden), F32), sds((hidden, width), F32)),
+            in_specs=[vmem] * 4,
+            out_specs=[hbm] * 3,
             scratch_shapes=[pltpu.VMEM((RING, width, TILE), F32), pltpu.VMEM((RING, width, TILE), F32),
-                            pltpu.VMEM((RING, TILE, width), F32), dma(()), dma((3, RING))],
+                            pltpu.VMEM((RING, TILE, width), F32), dma((3, RING))],
             cost_estimate=pl.CostEstimate(flops=6 * tokens * width * hidden, bytes_accessed=12 * width * hidden,
                                           transcendentals=0),
             compiler_params=pltpu.CompilerParams(vmem_limit_bytes=44 * 1024 * 1024),
-        )(x_t, dyc, hid, grad, y_own)
-        dx_new = pl.pallas_call(
+        )(x_t, dyc, hid, grad)
+        y_new, dx_new = pl.pallas_call(
             place_kernel,
-            name='place_dx',
-            out_shape=sds(own, BF16),
+            name='place_rows',
+            out_shape=(sds(own, BF16), sds(own, BF16)),
             in_specs=[vmem] * 4,
-            out_specs=vmem,
+            out_specs=[vmem] * 2,
             compiler_params=pltpu.CompilerParams(vmem_limit_bytes=4 * 1024 * 1024),
-        )(token_rows, dx_first, dx_half, dx_other)
+        )(token_rows, y_home, half_rows, other_rows)
         return y_new.reshape(rows, model), dx_new.reshape(rows, model), dw_gate, dw_up, dw_down
 
     row_spec = P('dp', None)

time: 80.3 us -> 78 us (0.971)
  Pallas kernels: 77.4 us -> 76.1 us
  starting transfers between devices: 1.04 us -> 0.03 us
    pallas_call x1, Pallas kernels: 64.1 us -> 62.8 us  [device_pass(): pl.pallas_call(exchange_kernel, name='exchange', out_shape=(sds((width, t...]
    ppermute x1, starting transfers between devices: 1.04 us -> 0.03 us  [device_pass(): other_rows = lax.ppermute(half_rows, 'tp', [(0, 1), (1, 0)])]
where the time goes in v6:
time: 78 us; the launch traced here: 77.9 us
  Pallas kernels  76.1 us (98%)
  other arithmetic  1.05 us (1%)
    pallas_call x1, Pallas kernels, device_pass(): pl.pallas_call(exchange_kernel, name='exchange', out_shape=(sds((width, t...  62.8 us
    pallas_call x1, Pallas kernels, device_pass(): pl.pallas_call(gradient_kernel, name='gradients', out_shape=(sds((width,...  12.6 us
  transfers between devices with their start and end apart: 1, of which 0 were waited for; matrix products, arithmetic and copies ran while one was open for 0% of the time, Pallas kernels for 16%

profile of v6, /device:TPU:0, one launch (start us, length us, event | category | flops | bytes accessed | tf_op | source)
XLA Modules:
  0.0 77.9 jit_solution(15640582702719827867)
XLA Ops:
  0.6 1.0 %pad_maximum_fusion = bf16[64,3072]{1,0:T(8,128)(2,1)S(1)} fusion(bf16[32,3072]{1,0:T(8,128)(2,1)} %param.9, bf16[32,3072]{1,0:T(8,128)(2,1)} %param.5), kind=kLoop, calls=%fused_computation | loop fusion | flops 786432 | bytes 786432 | tf_op jit(solution)/shard_map/concatenate | solution.py:425
  1.7 62.8 %exchange.1 = (bf16[768,128]{1,0:T(8,128)(2,1)S(1)}, bf16[2,4,16,768]{3,2,1,0:T(8,128)(2,1)S(1)}, bf16[4,2,4,16,1024]{4,3,2,1,0:T(8,128)(2,1)S(1)}, bf16[8,2,4,2...) custom-call(bf16[2,2,16,3072]{3,2,1,0:T(8,128)(2,1)S(1)} %bitcast.3, ...), custom_call_target="tpu_custom_call" | custom-call | tf_op jit(solution)/shard_map/exchange/pallas_call | solution.py:426
  64.4 0.0 collective-permute-start
  64.5 12.6 %gradients.1 = (f32[768,4096]{1,0:T(8,128)}, f32[768,4096]{1,0:T(8,128)}, f32[4096,768]{1,0:T(8,128)}) custom-call(bf16[768,128]{1,0:T(8,128)(2,1)S(1)} %get-tuple-element.20.x_t, bf16[2,4,16,768]{3,2,1,0:T(8,128)(2,1)S(1)} %get-tuple-element.21.dyc, bf16[4,2,4,16,1024]{4,3,2,1,0:T(8,128)(2,1)S(1)} %get-tuple-element.22.hid, ...), custom_call_target="tpu_custom_call" | custom-call | flops 2415919104 | bytes 37748736 | tf_op jit(solution)/shard_map/gradients/pallas_call | solution.py:454
  77.1 0.0 collective-permute-done.theirs
  77.1 0.8 %place_rows.1 = (bf16[2,16,3072]{2,1,0:T(8,128)(2,1)}, bf16[2,16,3072]{2,1,0:T(8,128)(2,1)}) custom-call(bf16[2,2,16,3072]{3,2,1,0:T(8,128)(2,1)S(1)} %bitcast.4, bf16[2,2,16,768]{3,2,1,0:T(8,128)(2,1)S(1)} %get-tuple-element.16.y_home, f32[8,16,768]{2,1,0:T(8,128)S(1)} %get-tuple-element.17.mine, f32[8,16,768]{2,1,0:T(8,128)S(1)} %collective-permute-done.theirs), custom_call_target="tpu_custom_call" | custom-call | tf_op jit(solution)/shard_map/place_rows/pallas_call | solution.py:466
Async XLA Ops:
  64.4 12.6 %collective-permute-start = (f32[8,16,768]{2,1,0:T(8,128)S(1)}, f32[8,16,768]{2,1,0:T(8,128)S(1)}, u32[]{:S(2)}, u32[]{:S(2)}) collective-permute-start(f32[8,16,768]{2,1,0:T(8,128)S(1)} %get-tuple-element.17.mine), channel_id=1, source_target_pairs={{0,4},{4,0},{1,5},{5,1},{2,6},{6,2},{3,7},{7,3}} | collective-permute-start | bytes 1179656 | tf_op jit(solution)/shard_map/ppermute | solution.py:452

commit v7 on v6

--- a/solution.py
+++ b/solution.py
@@ -25,7 +25,7 @@
 
 def exchange_kernel(token_rows, gate_hbm, up_hbm, down_hbm,
                     x_t, dyc, hid, grad, y_home, half_rows,
-                    xc, gate_up, down,
+                    xc, gate_up, down, last_t,
                     ab_keep, ab_give, ab_got, g_keep, g_give, g_got, ab_recv, g_recv,
                     y_acc, dx_away, dx_home, y_peer, dx_peer, y_sum, dx_sum, y_far, dx_far,
                     send, gate_up_sem, down_sem, tok_rs, core_rs, away_rs, link_rs,
@@ -60,10 +60,8 @@
     tokens = ((token_rows.at[0], xc), (token_rows.at[1], dyc))
     dy_own = token_rows.at[1]
     barrier = pltpu.get_barrier_semaphore()
-    for p in (FAR, SIB, DIAG):
-        pl.semaphore_signal(barrier, inc=1, device_id={'dp': peers[p]}, device_id_type=MESH)
-        pl.semaphore_signal(barrier, inc=1, device_id={'dp': peers[p], 'tp': 1 - tp}, device_id_type=MESH)
-    pl.semaphore_signal(barrier, inc=1, device_id={'tp': 1 - tp}, device_id_type=MESH)
+    for device in ({'dp': far}, {'dp': diag}, {'dp': sib}, {'tp': 1 - tp}, {'dp': sib, 'tp': 1 - tp}):
+        pl.semaphore_signal(barrier, inc=1, device_id=device, device_id_type=MESH)
     for g in range(groups):
         for s in (0, 1):
             for copy in load_gate_up(g, s):
@@ -72,7 +70,7 @@
         load_down(g).start()
     for own, slots in tokens:
         slots[:, OWN] = own[:, :, cols(dp)]
-    pl.semaphore_wait(barrier, 2 * SHARDS - 1)
+    pl.semaphore_wait(barrier, 5)
 
     def token(p, i):
         own, slots = tokens[i]
@@ -178,6 +176,8 @@
     token_fwd(1).wait_recv()
     each(lambda g: [part_g(1, g, s) for s in (0, 1)])
     x_t[...] = xc[...].reshape(2 * SHARDS * half, width).T
+    for i in (0, 1):
+        last_t[i] = gate_up[groups - 1, 1, i].T
 
     def hid_far(g):
         return remote(hid.at[g, :, FAR], hid.at[g, :, OWN], S_HID_FAR, hid_rs.at[0, g], dp=far)
@@ -205,11 +205,11 @@
         part = _dot(hid[g, :, 2 * q:2 * q + 2].reshape(4 * half, GROUP), down[g], 1, 0)
         y_acc[q] += part.reshape(y_acc.shape[1:])
 
-    def add_dx(acc, q, g, s):
+    def add_dx(acc, q, g, s, last=False):
         part = None
         for i in (0, 1):
             lhs = grad[2 * g + s, :, 2 * q:2 * q + 2, i].reshape(4 * half, CHUNK)
-            term = _dot(lhs, gate_up[g, s, i], 1, 1)
+            term = _dot(lhs, last_t[i], 1, 0) if last else _dot(lhs, gate_up[g, s, i], 1, 1)
             part = term if part is None else part + term
         acc[...] += part.reshape(acc.shape)
 
@@ -301,9 +301,9 @@
         grad_far(c).wait_recv()
         grad_fwd(c).start()
 
-    def home_dx(g, s):
+    def home_dx(g, s, last=False):
         grad_fwd(2 * g + s).wait_recv()
-        add_dx(dx_home, 0, g, s)
+        add_dx(dx_home, 0, g, s, last)
 
     def take_grads(g):
         take_grad(2 * g)
@@ -311,6 +311,9 @@
         @pl.when(g > 0)
         def _():
             home_dx(g - 1, 1)
+
+        take_grad(2 * g + 1)
+        home_dx(g, 0)
 
         @pl.when(g == 2)
         def _():
@@ -321,11 +324,8 @@
                     far_row(i, p).start()
             finish_y(0)
 
-        take_grad(2 * g + 1)
-        home_dx(g, 0)
-
     each(take_grads)
-    home_dx(groups - 1, 1)
+    home_dx(groups - 1, 1, last=True)
     swap().start()
     half_rows[0:2] = dx_home[:, 0]
     for p, r in home_rows:
@@ -434,6 +434,7 @@
             scratch_shapes=[
                 pltpu.VMEM(tok, BF16),
                 pltpu.VMEM((groups, 2, 2, width, CHUNK), BF16), pltpu.VMEM((groups, GROUP, width), BF16),
+                pltpu.VMEM((2, CHUNK, width), BF16),
                 pltpu.VMEM((2, chunks, 2, 2, half, CHUNK), F32), pltpu.VMEM((2, chunks, 2, 2, half, CHUNK), F32),
                 pltpu.VMEM((2, chunks, 2, 2, half, CHUNK), F32),
                 pltpu.VMEM((2, chunks, 2, half, CHUNK), F32), pltpu.VMEM((2, chunks, 2, half, CHUNK), F32),

time: 78 us -> 77.7 us (level)
  no operation moved by 1% of the time
where the time goes in v7:
time: 77.7 us; the launch traced here: 77.6 us
  Pallas kernels  75.7 us (97%)
  other arithmetic  1.05 us (1%)
    pallas_call x1, Pallas kernels, device_pass(): pl.pallas_call(exchange_kernel, name='exchange', out_shape=(sds((width, t...  62.4 us
    pallas_call x1, Pallas kernels, device_pass(): pl.pallas_call(gradient_kernel, name='gradients', out_shape=(sds((width,...  12.6 us
  transfers between devices with their start and end apart: 1, of which 0 were waited for; matrix products, arithmetic and copies ran while one was open for 0% of the time, Pallas kernels for 16%

profile of v7, /device:TPU:0, one launch (start us, length us, event | category | flops | bytes accessed | tf_op | source)
XLA Modules:
  0.0 77.6 jit_solution(17152538813198173341)
XLA Ops:
  0.6 1.0 %pad_maximum_fusion = bf16[64,3072]{1,0:T(8,128)(2,1)S(1)} fusion(bf16[32,3072]{1,0:T(8,128)(2,1)} %param.9, bf16[32,3072]{1,0:T(8,128)(2,1)} %param.5), kind=kLoop, calls=%fused_computation | loop fusion | flops 786432 | bytes 786432 | tf_op jit(solution)/shard_map/concatenate | solution.py:425
  1.7 62.4 %exchange.1 = (bf16[768,128]{1,0:T(8,128)(2,1)S(1)}, bf16[2,4,16,768]{3,2,1,0:T(8,128)(2,1)S(1)}, bf16[4,2,4,16,1024]{4,3,2,1,0:T(8,128)(2,1)S(1)}, bf16[8,2,4,2...) custom-call(bf16[2,2,16,3072]{3,2,1,0:T(8,128)(2,1)S(1)} %bitcast.3, ...), custom_call_target="tpu_custom_call" | custom-call | tf_op jit(solution)/shard_map/exchange/pallas_call | solution.py:426
  64.0 0.2 collective-permute-start
  64.2 12.6 %gradients.1 = (f32[768,4096]{1,0:T(8,128)}, f32[768,4096]{1,0:T(8,128)}, f32[4096,768]{1,0:T(8,128)}) custom-call(bf16[768,128]{1,0:T(8,128)(2,1)S(1)} %get-tuple-element.20.x_t, bf16[2,4,16,768]{3,2,1,0:T(8,128)(2,1)S(1)} %get-tuple-element.21.dyc, bf16[4,2,4,16,1024]{4,3,2,1,0:T(8,128)(2,1)S(1)} %get-tuple-element.22.hid, ...), custom_call_target="tpu_custom_call" | custom-call | flops 2415919104 | bytes 37748736 | tf_op jit(solution)/shard_map/gradients/pallas_call | solution.py:455
  76.8 0.0 collective-permute-done.theirs
  76.8 0.8 %place_rows.1 = (bf16[2,16,3072]{2,1,0:T(8,128)(2,1)}, bf16[2,16,3072]{2,1,0:T(8,128)(2,1)}) custom-call(bf16[2,2,16,3072]{3,2,1,0:T(8,128)(2,1)S(1)} %bitcast.4, bf16[2,2,16,768]{3,2,1,0:T(8,128)(2,1)S(1)} %get-tuple-element.16.y_home, f32[8,16,768]{2,1,0:T(8,128)S(1)} %get-tuple-element.17.mine, f32[8,16,768]{2,1,0:T(8,128)S(1)} %collective-permute-done.theirs), custom_call_target="tpu_custom_call" | custom-call | tf_op jit(solution)/shard_map/place_rows/pallas_call | solution.py:467
Async XLA Ops:
  64.0 12.8 %collective-permute-start = (f32[8,16,768]{2,1,0:T(8,128)S(1)}, f32[8,16,768]{2,1,0:T(8,128)S(1)}, u32[]{:S(2)}, u32[]{:S(2)}) collective-permute-start(f32[8,16,768]{2,1,0:T(8,128)S(1)} %get-tuple-element.17.mine), channel_id=1, source_target_pairs={{0,4},{4,0},{1,5},{5,1},{2,6},{6,2},{3,7},{7,3}} | collective-permute-start | bytes 1179656 | tf_op jit(solution)/shard_map/ppermute | solution.py:453

commit v8 on v7

--- a/solution.py
+++ b/solution.py
@@ -16,7 +16,8 @@
 OWN, SIB, FAR, DIAG = 0, 1, 2, 3
 (S_TOK, S_TOK_FWD, S_CORE_AB, S_CORE_G, S_LINK_AB, S_LINK_G, S_HID_FAR, S_HID_SIB, S_HID_FWD, S_GRAD_FAR, S_GRAD_SIB,
  S_GRAD_FWD, S_TP, S_ROW_HOME, S_ROW_AWAY, S_SWAP) = (0, 2, 4, 6, 8, 9, 10, 11, 12, 13, 14, 15, 16, 19, 20, 22)
-SENDS = 23
+SEND_SLOT = (0, 0, 0, 0, 0, 1, 0, 2, 0, 0, 0, 0, 0, 0, 3, 0, 4, 5, 6, 0, 7, 8, 9)
+SENDS = 10
 
 
 def _dot(lhs, rhs, lhs_dim, rhs_dim):
@@ -40,7 +41,7 @@
     groups = hid.shape[0]
 
     def remote(src, dst, ss, rs, **device):
-        return pltpu.make_async_remote_copy(src_ref=src, dst_ref=dst, send_sem=send.at[ss], recv_sem=rs,
+        return pltpu.make_async_remote_copy(src_ref=src, dst_ref=dst, send_sem=send.at[SEND_SLOT[ss]], recv_sem=rs,
                                             device_id=device, device_id_type=MESH)
 
     def cols(i):

time: 77.7 us -> 77.6 us (level)
  no operation moved by 1% of the time
where the time goes in v8:
time: 77.6 us; the launch traced here: 77.5 us
  Pallas kernels  75.6 us (97%)
  other arithmetic  1.05 us (1%)
    pallas_call x1, Pallas kernels, device_pass(): pl.pallas_call(exchange_kernel, name='exchange', out_shape=(sds((width, t...  62.2 us
    pallas_call x1, Pallas kernels, device_pass(): pl.pallas_call(gradient_kernel, name='gradients', out_shape=(sds((width,...  12.6 us
  transfers between devices with their start and end apart: 1, of which 0 were waited for; matrix products, arithmetic and copies ran while one was open for 0% of the time, Pallas kernels for 16%

profile of v8, /device:TPU:0, one launch (start us, length us, event | category | flops | bytes accessed | tf_op | source)
XLA Modules:
  0.0 77.5 jit_solution(14612053079972661354)
XLA Ops:
  0.6 1.0 %pad_maximum_fusion = bf16[64,3072]{1,0:T(8,128)(2,1)S(1)} fusion(bf16[32,3072]{1,0:T(8,128)(2,1)} %param.9, bf16[32,3072]{1,0:T(8,128)(2,1)} %param.5), kind=kLoop, calls=%fused_computation | loop fusion | flops 786432 | bytes 786432 | tf_op jit(solution)/shard_map/concatenate | solution.py:426
  1.7 62.2 %exchange.1 = (bf16[768,128]{1,0:T(8,128)(2,1)S(1)}, bf16[2,4,16,768]{3,2,1,0:T(8,128)(2,1)S(1)}, bf16[4,2,4,16,1024]{4,3,2,1,0:T(8,128)(2,1)S(1)}, bf16[8,2,4,2...) custom-call(bf16[2,2,16,3072]{3,2,1,0:T(8,128)(2,1)S(1)} %bitcast.3, ...), custom_call_target="tpu_custom_call" | custom-call | tf_op jit(solution)/shard_map/exchange/pallas_call | solution.py:427
  63.9 0.2 collective-permute-start
  64.1 12.6 %gradients.1 = (f32[768,4096]{1,0:T(8,128)}, f32[768,4096]{1,0:T(8,128)}, f32[4096,768]{1,0:T(8,128)}) custom-call(bf16[768,128]{1,0:T(8,128)(2,1)S(1)} %get-tuple-element.20.x_t, bf16[2,4,16,768]{3,2,1,0:T(8,128)(2,1)S(1)} %get-tuple-element.21.dyc, bf16[4,2,4,16,1024]{4,3,2,1,0:T(8,128)(2,1)S(1)} %get-tuple-element.22.hid, ...), custom_call_target="tpu_custom_call" | custom-call | flops 2415919104 | bytes 37748736 | tf_op jit(solution)/shard_map/gradients/pallas_call | solution.py:456
  76.7 0.0 collective-permute-done.theirs
  76.7 0.8 %place_rows.1 = (bf16[2,16,3072]{2,1,0:T(8,128)(2,1)}, bf16[2,16,3072]{2,1,0:T(8,128)(2,1)}) custom-call(bf16[2,2,16,3072]{3,2,1,0:T(8,128)(2,1)S(1)} %bitcast.4, bf16[2,2,16,768]{3,2,1,0:T(8,128)(2,1)S(1)} %get-tuple-element.16.y_home, f32[8,16,768]{2,1,0:T(8,128)S(1)} %get-tuple-element.17.mine, f32[8,16,768]{2,1,0:T(8,128)S(1)} %collective-permute-done.theirs), custom_call_target="tpu_custom_call" | custom-call | tf_op jit(solution)/shard_map/place_rows/pallas_call | solution.py:468
Async XLA Ops:
  63.9 12.8 %collective-permute-start = (f32[8,16,768]{2,1,0:T(8,128)S(1)}, f32[8,16,768]{2,1,0:T(8,128)S(1)}, u32[]{:S(2)}, u32[]{:S(2)}) collective-permute-start(f32[8,16,768]{2,1,0:T(8,128)S(1)} %get-tuple-element.17.mine), channel_id=1, source_target_pairs={{0,4},{4,0},{1,5},{5,1},{2,6},{6,2},{3,7},{7,3}} | collective-permute-start | bytes 1179656 | tf_op jit(solution)/shard_map/ppermute | solution.py:454

commit v9 on v8

--- a/solution.py
+++ b/solution.py
@@ -56,7 +56,7 @@
                 pltpu.make_async_copy(up_hbm.at[:, chunk_of(g, s)], gate_up.at[g, s, 1], sem))
 
     def load_down(g):
-        return pltpu.make_async_copy(down_hbm.at[pl.ds(pl.multiple_of(g * GROUP, GROUP), GROUP)], down.at[g], down_sem.at[g])
+        return pltpu.make_async_copy(down_hbm.at[pl.ds(pl.multiple_of(g * GROUP, GROUP), GROUP)], down.at[g], down_sem)
 
     tokens = ((token_rows.at[0], xc), (token_rows.at[1], dyc))
     dy_own = token_rows.at[1]
@@ -131,8 +131,6 @@
 
     def part_g(q, g, s):
         c = 2 * g + s
-        if q == 0 and s == 0:
-            load_down(g).wait()
         g_keep[q, c], g_give[q, c] = split(_dot(pair_rows(dyc, q), down[g, s * CHUNK:(s + 1) * CHUNK], 1, 1))
         core_g(q, c).start()
 
@@ -171,6 +169,7 @@
         tokens_far(i).wait_recv()
         token_fwd(i).start()
     token(SIB, 1).wait_recv()
+    pltpu.make_async_copy(down, down, down_sem).wait()
     home_parts(part_g, send_g, ((),))
     token_fwd(0).wait_recv()
     each(lambda g: [part_ab(1, g, s, i) for s in (0, 1) for i in (0, 1)])
@@ -253,7 +252,7 @@
         device = {} if p == OWN else {'dp': sib}
         if r:
             device['tp'] = 1 - tp
-        return remote(y_sum.at[p], y_home.at[p, r], S_ROW_HOME, home_rs.at[2 if p == OWN else r], **device)
+        return remote(y_sum.at[p], y_home.at[p, r], S_ROW_HOME, home_rs, **device)
 
     home_rows = ((OWN, 1), (SIB, 0), (SIB, 1))
 
@@ -329,8 +328,7 @@
     home_dx(groups - 1, 1, last=True)
     swap().start()
     half_rows[0:2] = dx_home[:, 0]
-    for p, r in home_rows:
-        row_home(p, r).wait_recv()
+    remote(y_sum.at[0:3], y_sum.at[0:3], S_ROW_HOME, home_rs, dp=sib).wait_recv()
 
     for i in (0, 1):
         slots = tokens[i][1]
@@ -344,7 +342,7 @@
         remote(hid.at[:, :, OWN], hid.at[:, :, SIB], kind, hid_rs.at[0, 0], dp=sib).wait_send()
     for kind in (S_GRAD_FAR, S_GRAD_FWD):
         remote(grad.at[:, :, OWN], grad.at[:, :, SIB], kind, grad_sib_rs, dp=sib).wait_send()
-    remote(y_sum.at[0:3], y_sum.at[0:3], S_ROW_HOME, home_rs.at[0], dp=sib).wait_send()
+    remote(y_sum.at[0:3], y_sum.at[0:3], S_ROW_HOME, home_rs, dp=sib).wait_send()
 
     for i, rows_in in enumerate((y_far, dx_far)):
         far_rows(i).wait()
@@ -445,8 +443,8 @@
                 pltpu.VMEM((2,) + block, F32), pltpu.VMEM(block, F32),
                 pltpu.VMEM((SHARDS, half, width), BF16), pltpu.VMEM(block, BF16),
                 pltpu.VMEM(block, BF16), pltpu.VMEM(block, BF16),
-                dma((SENDS,)), dma((chunks,)), dma((groups,)), dma((2, 3)), dma((2, 4)), dma((2,)),
-                dma((2, groups)), dma((3, groups)), dma((2, chunks)), dma(()), dma((3,)), dma((3,)), dma((2,)), dma(()),
+                dma((SENDS,)), dma((chunks,)), dma(()), dma((2, 3)), dma((2, 4)), dma((2,)),
+                dma((2, groups)), dma((3, groups)), dma((2, chunks)), dma(()), dma((3,)), dma(()), dma((2,)), dma(()),
             ],
             compiler_params=pltpu.CompilerParams(collective_id=0, has_side_effects=True,
                                                  vmem_limit_bytes=44 * 1024 * 1024),

time: 77.6 us -> 77.6 us (level)
  no operation moved by 1% of the time
where the time goes in v9:
time: 77.6 us; the launch traced here: 77.5 us
  Pallas kernels  75.6 us (97%)
  other arithmetic  1.05 us (1%)
    pallas_call x1, Pallas kernels, device_pass(): pl.pallas_call(exchange_kernel, name='exchange', out_shape=(sds((width, t...  62.2 us
    pallas_call x1, Pallas kernels, device_pass(): pl.pallas_call(gradient_kernel, name='gradients', out_shape=(sds((width,...  12.6 us
  transfers between devices with their start and end apart: 1, of which 0 were waited for; matrix products, arithmetic and copies ran while one was open for 0% of the time, Pallas kernels for 16%

profile of v9, /device:TPU:0, one launch (start us, length us, event | category | flops | bytes accessed | tf_op | source)
XLA Modules:
  0.0 77.5 jit_solution(4852688158993857875)
XLA Ops:
  0.6 1.0 %pad_maximum_fusion = bf16[64,3072]{1,0:T(8,128)(2,1)S(1)} fusion(bf16[32,3072]{1,0:T(8,128)(2,1)} %param.9, bf16[32,3072]{1,0:T(8,128)(2,1)} %param.5), kind=kLoop, calls=%fused_computation | loop fusion | flops 786432 | bytes 786432 | tf_op jit(solution)/shard_map/concatenate | solution.py:424
  1.7 62.2 %exchange.1 = (bf16[768,128]{1,0:T(8,128)(2,1)S(1)}, bf16[2,4,16,768]{3,2,1,0:T(8,128)(2,1)S(1)}, bf16[4,2,4,16,1024]{4,3,2,1,0:T(8,128)(2,1)S(1)}, bf16[8,2,4,2...) custom-call(bf16[2,2,16,3072]{3,2,1,0:T(8,128)(2,1)S(1)} %bitcast.3, ...), custom_call_target="tpu_custom_call" | custom-call | tf_op jit(solution)/shard_map/exchange/pallas_call | solution.py:425
  63.9 0.2 collective-permute-start
  64.1 12.6 %gradients.1 = (f32[768,4096]{1,0:T(8,128)}, f32[768,4096]{1,0:T(8,128)}, f32[4096,768]{1,0:T(8,128)}) custom-call(bf16[768,128]{1,0:T(8,128)(2,1)S(1)} %get-tuple-element.20.x_t, bf16[2,4,16,768]{3,2,1,0:T(8,128)(2,1)S(1)} %get-tuple-element.21.dyc, bf16[4,2,4,16,1024]{4,3,2,1,0:T(8,128)(2,1)S(1)} %get-tuple-element.22.hid, ...), custom_call_target="tpu_custom_call" | custom-call | flops 2415919104 | bytes 37748736 | tf_op jit(solution)/shard_map/gradients/pallas_call | solution.py:454
  76.6 0.0 collective-permute-done.theirs
  76.7 0.8 %place_rows.1 = (bf16[2,16,3072]{2,1,0:T(8,128)(2,1)}, bf16[2,16,3072]{2,1,0:T(8,128)(2,1)}) custom-call(bf16[2,2,16,3072]{3,2,1,0:T(8,128)(2,1)S(1)} %bitcast.4, bf16[2,2,16,768]{3,2,1,0:T(8,128)(2,1)S(1)} %get-tuple-element.16.y_home, f32[8,16,768]{2,1,0:T(8,128)S(1)} %get-tuple-element.17.mine, f32[8,16,768]{2,1,0:T(8,128)S(1)} %collective-permute-done.theirs), custom_call_target="tpu_custom_call" | custom-call | tf_op jit(solution)/shard_map/place_rows/pallas_call | solution.py:466
Async XLA Ops:
  63.9 12.8 %collective-permute-start = (f32[8,16,768]{2,1,0:T(8,128)S(1)}, f32[8,16,768]{2,1,0:T(8,128)S(1)}, u32[]{:S(2)}, u32[]{:S(2)}) collective-permute-start(f32[8,16,768]{2,1,0:T(8,128)S(1)} %get-tuple-element.17.mine), channel_id=1, source_target_pairs={{0,4},{4,0},{1,5},{5,1},{2,6},{6,2},{3,7},{7,3}} | collective-permute-start | bytes 1179656 | tf_op jit(solution)/shard_map/ppermute | solution.py:452
